TPU v7x, 32 devices: a 4x4x1 block of a 4x4x8 slice. The times are simulated.
32 devices in a mesh: pair: 1 (over z), tp: 4 (over y), side: 8 (over x, core).
Axes of the slice: x: 4, y: 4, z: 1, core: 2. Of those that a mesh axis runs over, the one named last changes fastest.
The devices are a block of a 4x4x8 slice.
Arguments:
- prompt_x: bfloat16 [8192, 2560], P(('pair', 'side'))
- s_len: int32 [8], P(('pair', 'side'))
- w_qkv_pre: bfloat16 [1, 2560, 3, 20, 128], P(None, None, None, 'tp')
- w_out_pre: bfloat16 [1, 20, 128, 2560], P(None, 'tp')
- w_gu_pre: bfloat16 [1, 2, 6912, 2560], P(None, None, 'tp')
- w_down_pre: bfloat16 [1, 6912, 2560], P(None, 'tp')
- gain_pre: float32 [1, 2, 2560], replicated
- dec_tokens: bfloat16 [128, 2560], P(('pair', 'side'))
- k_cache: bfloat16 [1, 128, 256, 5, 4, 128], P(None, ('pair', 'side'), None, None, 'tp')
- v_cache: bfloat16 [1, 128, 256, 5, 4, 128], P(None, ('pair', 'side'), None, None, 'tp')
- c_len: int32 [128], P(('pair', 'side'))
- w_qkv_dec: bfloat16 [1, 2560, 3, 5, 4, 128], P(None, None, None, None, 'tp')
- w_out_dec: bfloat16 [1, 5, 4, 128, 2560], P(None, None, 'tp')
- w_gu_dec: bfloat16 [1, 2, 6912, 2560], P(None, None, 'tp')
- w_down_dec: bfloat16 [1, 6912, 2560], P(None, 'tp')
- gain_dec: float32 [1, 2, 2560], replicated
Outputs:
- output 1: bfloat16 [8192, 2560], P(('pair', 'side'))
- output 2: bfloat16 [128, 2560], P(('pair', 'side'))
- output 3: bfloat16 [1, 8192, 5, 4, 128], P(None, ('pair', 'side'), None, 'tp')
- output 4: bfloat16 [1, 8192, 5, 4, 128], P(None, ('pair', 'side'), None, 'tp')
- output 5: bfloat16 [1, 128, 256, 5, 4, 128], P(None, ('pair', 'side'), None, None, 'tp')
- output 6: bfloat16 [1, 128, 256, 5, 4, 128], P(None, ('pair', 'side'), None, None, 'tp')
All inputs are finite; a program needn't handle non-finite values.
Results may differ from a plain program's by a relative error of at most 0.0126162.
Values are sent between devices in bfloat16 or wider.
A program may use at most 768 MiB of HBM per device.

v0:
```python
import jax
import jax.numpy as jnp
from jax import lax
from jax.sharding import PartitionSpec as P

EPSILON = 1e-6
THETA = 10000.0
MASKED = -1e30


def rms_norm(hidden, gain_vec):
    hid_f32 = hidden.astype(jnp.float32)
    inv_rms = lax.rsqrt(jnp.mean(hid_f32 * hid_f32, axis=-1, keepdims=True) + EPSILON)
    return (hid_f32 * inv_rms * gain_vec).astype(jnp.bfloat16)


def add_residual(hidden, update):
    return (hidden.astype(jnp.float32) + update.astype(jnp.float32)).astype(jnp.bfloat16)


def rope_tables(positions, head_dim):
    half_dim = head_dim // 2
    inv_freq = THETA ** (-jnp.arange(half_dim, dtype=jnp.float32) * 2.0 / head_dim)
    angles = positions.astype(jnp.float32)[:, None] * inv_freq[None, :]
    return jnp.cos(angles), jnp.sin(angles)


def apply_rope(values_in, cos_tab, sin_tab):
    half_dim = values_in.shape[-1] // 2
    lower_half = values_in[..., :half_dim]
    upper_half = values_in[..., half_dim:]
    cos_b = cos_tab[:, None, :]
    sin_b = sin_tab[:, None, :]
    return jnp.concatenate([lower_half * cos_b - upper_half * sin_b, upper_half * cos_b + lower_half * sin_b], axis=-1)


def swiglu(hidden, gain_vec, w_gu, w_down):
    normed = rms_norm(hidden, gain_vec)
    gate_up = jnp.einsum('...d,kfd->...kf', normed, w_gu, preferred_element_type=jnp.float32)
    gate_val = gate_up[..., 0, :].astype(jnp.bfloat16).astype(jnp.float32)
    up_val = gate_up[..., 1, :].astype(jnp.bfloat16).astype(jnp.float32)
    activated = (jax.nn.silu(gate_val) * up_val).astype(jnp.bfloat16)
    return jnp.einsum('...f,fd->...d', activated, w_down, preferred_element_type=jnp.float32)


def prompt_attention(queries, keys_in, values_in, allowed):
    attn_scale = queries.shape[-1] ** -0.5
    scores = jnp.einsum('nqhe,nkhe->nhqk', queries, keys_in, preferred_element_type=jnp.float32) * attn_scale
    scores = jnp.where(allowed[:, None], scores, MASKED)
    prob_bf = jax.nn.softmax(scores, axis=-1).astype(jnp.bfloat16)
    return jnp.einsum('nhqk,nkhe->nqhe', prob_bf, values_in, preferred_element_type=jnp.float32).astype(jnp.bfloat16)


def decode_attention(queries, k_tok, v_tok, k_layer, v_layer, visible):
    attn_scale = queries.shape[-1] ** -0.5
    cache_scores = jnp.einsum('bhe,bthe->bht', queries, k_layer, preferred_element_type=jnp.float32) * attn_scale
    cache_scores = jnp.where(visible, cache_scores, MASKED)
    self_score = jnp.einsum('bhe,bhe->bh', queries, k_tok, preferred_element_type=jnp.float32) * attn_scale
    row_max = jnp.maximum(jnp.max(cache_scores, axis=-1), self_score)
    cache_exp = jnp.exp(cache_scores - row_max[..., None])
    self_exp = jnp.exp(self_score - row_max)
    denominator = jnp.sum(cache_exp, axis=-1) + self_exp
    cache_prob = (cache_exp / denominator[..., None]).astype(jnp.bfloat16)
    self_prob = (self_exp / denominator).astype(jnp.bfloat16).astype(jnp.float32)
    context = jnp.einsum('bht,bthe->bhe', cache_prob, v_layer, preferred_element_type=jnp.float32) + self_prob[..., None] * v_tok.astype(jnp.float32)
    return context.astype(jnp.bfloat16)


def run_prefill(prompts, s_valid, w_qkv, w_out, w_gu, w_down, gains):
    seq_len = prompts.shape[1]
    positions = jnp.arange(seq_len)
    cos_tab, sin_tab = rope_tables(positions, w_qkv.shape[-1])
    allowed = (positions[None, :] <= positions[:, None])[None] & (positions[None, None, :] < s_valid[:, None, None])
    hidden = prompts
    kv_layers = []
    for layer_idx in range(w_qkv.shape[0]):
        normed = rms_norm(hidden, gains[layer_idx, 0])
        qkv_out = jnp.einsum('nsd,dkhe->nskhe', normed, w_qkv[layer_idx], preferred_element_type=jnp.float32)
        queries = apply_rope(qkv_out[:, :, 0], cos_tab, sin_tab).astype(jnp.bfloat16)
        keys_new = apply_rope(qkv_out[:, :, 1], cos_tab, sin_tab).astype(jnp.bfloat16)
        values_new = qkv_out[:, :, 2].astype(jnp.bfloat16)
        context = prompt_attention(queries, keys_new, values_new, allowed)
        part_sum = jnp.einsum('nshe,hed->nsd', context, w_out[layer_idx], preferred_element_type=jnp.float32)
        hidden = add_residual(hidden, lax.psum(part_sum, 'tp').astype(jnp.bfloat16))
        mlp_part = swiglu(hidden, gains[layer_idx, 1], w_gu[layer_idx], w_down[layer_idx])
        hidden = add_residual(hidden, lax.psum(mlp_part, 'tp').astype(jnp.bfloat16))
        kv_layers.append(jnp.stack([keys_new, values_new]))
    return hidden, kv_layers


def run_decode(tokens, k_cache, v_cache, c_len, w_qkv, w_out, w_gu, w_down, gains):
    layers = k_cache.shape[0]
    row_count = k_cache.shape[1]
    cache_len = k_cache.shape[2]
    heads_loc = k_cache.shape[3]
    head_dim = k_cache.shape[5]
    model_width = tokens.shape[1]
    k_local = k_cache.reshape(layers, row_count, cache_len, heads_loc, head_dim)
    v_local = v_cache.reshape(layers, row_count, cache_len, heads_loc, head_dim)
    wqkv_local = w_qkv.reshape(layers, model_width, 3, heads_loc, head_dim)
    wout_local = w_out.reshape(layers, heads_loc, head_dim, model_width)
    cos_tab, sin_tab = rope_tables(c_len, head_dim)
    cache_pos = jnp.arange(cache_len)
    visible = (cache_pos[None, :] < c_len[:, None])[:, None, :]
    write_at = (cache_pos[None, :] == c_len[:, None])[:, :, None, None]
    k_next = []
    v_next = []
    for layer_idx in range(layers):
        normed = rms_norm(tokens, gains[layer_idx, 0])
        qkv_out = jnp.einsum('bd,dkhe->bkhe', normed, wqkv_local[layer_idx], preferred_element_type=jnp.float32)
        queries = apply_rope(qkv_out[:, 0], cos_tab, sin_tab).astype(jnp.bfloat16)
        k_tok = apply_rope(qkv_out[:, 1], cos_tab, sin_tab).astype(jnp.bfloat16)
        v_tok = qkv_out[:, 2].astype(jnp.bfloat16)
        context = decode_attention(queries, k_tok, v_tok, k_local[layer_idx], v_local[layer_idx], visible)
        part_sum = jnp.einsum('bhe,hed->bd', context, wout_local[layer_idx], preferred_element_type=jnp.float32)
        tokens = add_residual(tokens, lax.psum(part_sum, 'tp').astype(jnp.bfloat16))
        mlp_part = swiglu(tokens, gains[layer_idx, 1], w_gu[layer_idx], w_down[layer_idx])
        tokens = add_residual(tokens, lax.psum(mlp_part, 'tp').astype(jnp.bfloat16))
        k_next.append(jnp.where(write_at, k_tok[:, None], k_local[layer_idx]))
        v_next.append(jnp.where(write_at, v_tok[:, None], v_local[layer_idx]))
    return tokens, jnp.stack(k_next).reshape(k_cache.shape), jnp.stack(v_next).reshape(v_cache.shape)


def heads_to_rows(kv_local, tp_size):
    pair_kv, seq_len, heads_loc, head_dim = kv_local.shape
    by_block = kv_local.reshape(pair_kv, tp_size, seq_len // tp_size, heads_loc, head_dim)
    gathered = lax.all_to_all(by_block, 'tp', 1, 2)
    return gathered.reshape(pair_kv, seq_len // tp_size, tp_size * heads_loc, head_dim)


def rows_to_heads(kv_rows, tp_size):
    pair_kv, seq_part, heads_all, head_dim = kv_rows.shape
    grouped = kv_rows.reshape(pair_kv, seq_part, heads_all // tp_size, tp_size, head_dim)
    spread = lax.all_to_all(grouped, 'tp', 3, 1)
    return spread.reshape(pair_kv, tp_size * seq_part, heads_all // tp_size, head_dim)


def solution(mesh):
    tp_size = mesh.shape['tp']
    side_size = mesh.shape['side']
    partner_perm = [(src_idx, (src_idx + side_size // 2) % side_size) for src_idx in range(side_size)]
    inst_axes = ('pair', 'side')
    rows_spec = P(inst_axes, None)
    vec_spec = P(inst_axes)
    cache_spec = P(None, inst_axes, None, None, 'tp', None)
    prompt_spec = P(None, inst_axes, None, 'tp', None)
    in_specs = (rows_spec, vec_spec, P(None, None, None, 'tp', None), P(None, 'tp', None, None), P(None, None, 'tp', None), P(None, 'tp', None), P(None, None, None), rows_spec, cache_spec, cache_spec, vec_spec, P(None, None, None, None, 'tp', None), P(None, None, 'tp', None, None), P(None, None, 'tp', None), P(None, 'tp', None), P(None, None, None))
    out_specs = (rows_spec, rows_spec, prompt_spec, prompt_spec, cache_spec, cache_spec)

    def device_fn(prompt_x, s_len, w_qkv_pre, w_out_pre, w_gu_pre, w_down_pre, gain_pre, dec_tokens, k_cache, v_cache, c_len, w_qkv_dec, w_out_dec, w_gu_dec, w_down_dec, gain_dec):
        hidden, kv_layers = run_prefill(prompt_x[None], s_len, w_qkv_pre, w_out_pre, w_gu_pre, w_down_pre, gain_pre)
        installed = []
        for kv_layer in kv_layers:
            kv_rows = heads_to_rows(kv_layer[:, 0], tp_size)
            kv_rows = lax.ppermute(kv_rows, 'side', partner_perm)
            installed.append(rows_to_heads(kv_rows, tp_size))
        prompt_kv = jnp.stack(installed, axis=1)[:, :, :, :, None, :]
        dec_out, k_cache_new, v_cache_new = run_decode(dec_tokens, k_cache, v_cache, c_len, w_qkv_dec, w_out_dec, w_gu_dec, w_down_dec, gain_dec)
        return hidden[0], dec_out, prompt_kv[0], prompt_kv[1], k_cache_new, v_cache_new

    return jax.shard_map(device_fn, mesh=mesh, in_specs=in_specs, out_specs=out_specs, check_vma=False)
```

profile of v0, /device:TPU:96, one launch (start us, length us, event | category | flops | bytes accessed | tf_op | source)
XLA Modules:
  0.0 594.3 jit_solution(8940648248530262474)
XLA Ops:
  0.7 13.9 %copy.74 = bf16[2560,3,5,128]{0,3,2,1:T(8,128)(2,1)} copy(bf16[2560,3,5,128]{3,0,2,1:T(8,128)(2,1)} %bitcast.161) | data formatting | bytes 19660800 | tf_op jit(solution)/shard_map/squeeze | solution.py:78
  15.2 3.9 fusion.8
  19.1 13.2 %fusion.38 = f32[1024,1920]{0,1:S(1)} fusion(bf16[2560,1920]{0,1:T(8,128)(2,1)} %bitcast.162, bf16[1024,2560]{1,0:T(8,128)(2,1)S(1)} %copy-done.2, f32[2560]{0:T(1024)S(1)} %get-tuple-element.21, f32[1024]{0:T(1024)S(1)} %add_rsqrt_fusion.1), kind=kOutput, calls=%fused_computation.46 | convolution fusion | flops 10076815360 | bytes 22951936
  38.3 3.8 convert_element_type.265
  42.0 3.5 copy.81
  46.5 5.0 fusion.63
  61.1 4.4 pad_maximum_fusion
  65.6 5.3 all-to-all-start
  73.6 14.0 %fusion.113 = (f32[5,1024]{1,0:T(8,128)S(1)}, f32[5,1024,1024]{1,2,0:T(8,128)}) fusion(pred[1024,1024]{0,1:T(8,128)(4,1)} %fusion.48, bf16[1024,5,64]{0,2,1:T(8,128)(2,1)} %bitcast.166, bf16[1024,5,64]{0,2,1:T(8,128)(2,1)} %bitcast.167, bf16[1024,5,64]{0,2,1:T(8,128)(2,1)} %get-tuple-element.35, bf16[1024,5,64]{0,2,1:T(8,128)(2,1)} %get-tuple-element.34), kind=kOutput, calls=%fused_computation.164 | convolution fusion | flops 1368392704 | bytes 24662016 | tf_op jit(solution)/shard_map/sub | solution.py:50
  87.6 13.1 %convolution_bitcast_fusion = f32[1,1024,2560]{2,1,0:T(8,128)} fusion(bf16[1,5,128,2560]{3,2,1,0:T(8,128)(2,1)S(1)} %copy-done, f32[5,1024,1024]{1,2,0:T(8,128)} %get-tuple-element.61, f32[5,1024]{1,0:T(8,128)S(1)} %get-tuple-element.60, f32[1,1024,3,5,128]{1,4,3,2,0:T(8,128)} %bitcast.165), kind=kOutput, calls=%fused_computation.43 | convolution fusion | flops 4708761600 | bytes 36065280 | tf_op jit(solution)/shard_map/nshe,hed->nsd/dot_general | solution.py:83
  101.0 5.4 fusion.19
  106.8 4.1 fusion.42
  112.7 187.7 %all-reduce.4 = (bf16[1,1024,2560]{2,1,0:T(8,128)(2,1)}, bf16[16,2560]{1,0:T(8,128)(2,1)S(1)}) all-reduce(f32[1,1024,2560]{2,1,0:T(8,128)} %convolution_bitcast_fusion, f32[16,2560]{1,0:T(8,128)S(1)} %convolution_bitcast_fusion.1), channel_id=1, replica_groups=mesh['pair'=1,'tp'=4,'side'=8] {'tp'}, use_global_device_ids=true, to_apply=%region_3.4 | all-reduce | flops 2662400 | bytes 15974400 | tf_op jit(solution)/shard_map/psum | solution.py:84
  300.5 6.3 %fusion.11 = (f32[1024]{0:T(1024)S(1)}, bf16[1,1024,2560]{2,1,0:T(8,128)(2,1)S(1)}) fusion(bf16[1,1024,2560]{2,1,0:T(8,128)(2,1)} %get-tuple-element.24, bf16[1024,2560]{1,0:T(8,128)(2,1)} %param.16), kind=kLoop, calls=%fused_computation.20 | loop fusion | flops 18349056 | bytes 15732736 | tf_op jit(solution)/shard_map/reduce_sum | solution.py:13
  306.8 23.6 %convert_bitcast_fusion.1 = bf16[1,1024,2,1728]{1,3,2,0:T(8,128)(2,1)S(1)} fusion(bf16[1,2,1728,2560]{3,2,1,0:T(8,128)(2,1)} %param.20, bf16[1,1024,2560]{2,1,0:T(8,128)(2,1)S(1)} %get-tuple-element.29, f32[2560]{0:T(1024)S(1)} %copy-done.11, f32[1024]{0:T(1024)S(1)} %add_rsqrt_fusion), kind=kOutput, calls=%fused_computation.40 | convolution fusion | flops 18133417984 | bytes 30029824 | tf_op jit(solution)/shard_map/...d,kfd->...kf/dot_general | solution.py:39
  330.4 16.3 %fusion.30 = f32[1,1024,2560]{2,1,0:T(8,128)} fusion(bf16[1,1728,2560]{2,1,0:T(8,128)(2,1)} %param.21, bf16[1,1024,2,1728]{1,3,2,0:T(8,128)(2,1)S(1)} %convert_bitcast_fusion.1), kind=kOutput, calls=%fused_computation.42 | convolution fusion | flops 9073852416 | bytes 26411008 | tf_op jit(solution)/shard_map/...f,fd->...d/dot_general | solution.py:43
  346.9 10.7 %fusion.55 = bf16[16,2,1728]{2,0,1:T(8,128)(2,1)S(1)} fusion(bf16[1,2,1728,2560]{3,2,1,0:T(8,128)(2,1)} %param.29, bf16[16,2560]{1,0:T(8,128)(2,1)S(1)} %get-tuple-element.27, f32[2560]{0:T(1024)S(1)} %get-tuple-element.18, f32[16]{0:T(128)S(1)} %add_rsqrt_fusion.2), kind=kOutput, calls=%fused_computation.69 | convolution fusion | flops 283334656 | bytes 17897536 | tf_op jit(solution)/shard_map/...d,kfd->...kf/dot_general | solution.py:39
  357.6 4.8 fusion.21
  367.9 182.3 %all-reduce.5 = (bf16[1,1024,2560]{2,1,0:T(8,128)(2,1)}, bf16[16,2560]{1,0:T(8,128)(2,1)S(1)}) all-reduce(f32[1,1024,2560]{2,1,0:T(8,128)} %fusion.30, f32[16,2560]{1,0:T(8,128)S(1)} %fusion.21), channel_id=1, replica_groups=mesh['pair'=1,'tp'=4,'side'=8] {'tp'}, use_global_device_ids=true, to_apply=%region_5.6 | all-reduce | flops 2662400 | bytes 15974400 | tf_op jit(solution)/shard_map/psum | solution.py:86
  551.7 3.6 copy.83
  555.2 4.6 all-to-all-start.1
  559.9 9.0 %broadcast_select_fusion = (bf16[1,16,256,5,1,128]{5,2,4,3,1,0:T(8,128)(2,1)}, bf16[1,16,256,5,1,128]{5,2,4,3,1,0:T(8,128)(2,1)}) fusion(bf16[1,16,256,5,1,128]{5,2,4,3,1,0:T(8,128)(2,1)} %param.25, pred[16,256]{1,0:T(8,128)(4,1)S(1)} %copy-done.10, bf16[16,5,128]{2,1,0:T(8,128)(2,1)S(1)} %copy.86, bf16[1,16,256,5,1,128]{5,2,4,3,1,0:T(8,128)(2,1)} %param.24, ...), kind=kLoop, calls=%fused_computation.55 | loop fusion | flops 5242880 | bytes 21016576 | tf_op jit(solution)/shard_map/jit(_where)/select_n | solution.py:120
  568.9 7.9 %fusion.35 = bf16[1024,2560]{1,0:T(8,128)(2,1)} fusion(bf16[1,1024,2560]{2,1,0:T(8,128)(2,1)} %copy-done.3, bf16[1,1024,2560]{2,1,0:T(8,128)(2,1)} %get-tuple-element.22), kind=kLoop, calls=%fused_computation.44 | loop fusion | flops 10485760 | bytes 15728640 | tf_op jit(solution)/shard_map/squeeze | solution.py:159
  576.9 13.2 %all-to-all-done.1 = bf16[2,1,256,5,4,128]{5,2,3,0,1,4:T(8,128)(2,1)} async-done(((bf16[2,1,256,5,4,128]{5,2,3,0,1,4:T(8,128)(2,1)}), bf16[2,1,256,5,4,128]{5,2,3,0,1,4:T(8,128)(2,1)}, u32[]{:S(2)}, u32[]{:S(2)}) %all-to-all-start.1) | async-done | bytes 2621472 | tf_op jit(solution)/shard_map/all_to_all | solution.py:134
  (74 shorter events, 32.6 us)
Async XLA Ops:
  0.6 87.0 %copy-start = (bf16[1,5,128,2560]{3,2,1,0:T(8,128)(2,1)S(1)}, bf16[1,5,128,2560]{3,2,1,0:T(8,128)(2,1)}, u32[]{:S(2)}) copy-start(bf16[1,5,128,2560]{3,2,1,0:T(8,128)(2,1)} %param.19) | copy-start | bytes 9830404
  0.7 13.9 %copy-start.8 = (f32[1,2,2560]{2,1,0:T(2,128)S(1)}, f32[1,2,2560]{2,1,0:T(2,128)}, u32[]{:S(2)}) copy-start(f32[1,2,2560]{2,1,0:T(2,128)} %param.22) | copy-start | bytes 61444
  14.6 4.5 copy-start.2
  32.3 4.7 copy-start.4
  61.1 9.8 %copy-start.12 = (s32[16]{0:T(128)S(1)}, s32[16]{0:T(128)}, u32[]{:S(2)}) copy-start(s32[16]{0:T(128)} %param.26) | copy-start | bytes 196
  65.6 296.8 %all-to-all-start = ((bf16[2,4,256,1,5,128]{5,2,4,0,3,1:T(8,128)(2,1)}), bf16[2,4,256,1,5,128]{5,2,4,0,3,1:T(8,128)(2,1)}, u32[]{:S(2)}, u32[]{:S(2)}) async-start(bf16[2,4,256,1,5,128]{5,2,4,0,3,1:T(8,128)(2,1)} %pad_maximum_fusion), calls=%async_computation | async-start | bytes 5242880 | tf_op jit(solution)/shard_map/all_to_all | solution.py:127
  87.6 13.1 %copy-start.9 = (f32[1,2,2560]{2,1,0:T(2,128)S(1)}, f32[1,2,2560]{2,1,0:T(2,128)}, u32[]{:S(2)}) copy-start(f32[1,2,2560]{2,1,0:T(2,128)} %param.31) | copy-start | bytes 61444
  87.6 13.2 %copy-start.6 = (bf16[16,2560]{1,0:T(8,128)(2,1)S(1)}, bf16[16,2560]{1,0:T(8,128)(2,1)}, u32[]{:S(2)}) copy-start(bf16[16,2560]{1,0:T(8,128)(2,1)} %param.23) | copy-start | bytes 245764
  100.9 10.4 %slice-start = ((s8[5242880]{0:T(1024)(128)(4,1)}), s8[4194304]{0:T(1024)(128)(4,1)S(1)}, s32[]{:S(2)}) async-start(s8[5242880]{0:T(1024)(128)(4,1)} %bitcast.158), calls=%async_computation.2 | async-start | bytes 8388608
  101.0 10.4 %slice-start.1 = ((s8[5242880]{0:T(1024)(128)(4,1)}), s8[1048576]{0:T(1024)(128)(4,1)S(1)}, s32[]{:S(2)}) async-start(s8[5242880]{0:T(1024)(128)(4,1)} %bitcast.158), calls=%async_computation.3 | async-start | bytes 2097152
  106.3 5.8 copy-start.7
  106.8 5.3 copy-start.5
  300.5 6.3 %copy-start.11 = (f32[2560]{0:T(1024)S(1)}, f32[2560]{0:T(1024)}, u32[]{:S(2)}) copy-start(f32[2560]{0:T(1024)} %get-tuple-element.20) | copy-start | bytes 30724
  306.8 23.6 %copy-start.3 = (bf16[1,1024,2560]{2,1,0:T(8,128)(2,1)}, bf16[1,1024,2560]{2,1,0:T(8,128)(2,1)S(1)}, u32[]{:S(2)}) copy-start(bf16[1,1024,2560]{2,1,0:T(8,128)(2,1)S(1)} %get-tuple-element.29) | copy-start | bytes 15728644
  364.5 187.2 %collective-permute-start = (bf16[2,256,20,128]{3,1,2,0:T(8,128)(2,1)S(1)}, bf16[2,256,20,128]{3,1,2,0:T(8,128)(2,1)}, u32[]{:S(2)}, u32[]{:S(2)}) collective-permute-start(bf16[2,256,20,128]{3,1,2,0:T(8,128)(2,1)S(1)} %bitcast.168), channel_id=1, source_target_pairs={{0,4},{1,5},{2,6},{3,7},{4,0},{5,1},{6,2},{7,3},{8,12},{9,13},{10,... | collective-permute-start | bytes 7864328 | tf_op jit(solution)/shard_map/ppermute | solution.py:155
  551.7 8.2 %copy-start.10 = (pred[16,256]{1,0:T(8,128)(4,1)S(1)}, pred[16,256]{1,0:T(8,128)(4,1)}, u32[]{:S(2)}) copy-start(pred[16,256]{1,0:T(8,128)(4,1)} %get-tuple-element.58) | copy-start | bytes 12292
  555.2 34.8 %all-to-all-start.1 = ((bf16[2,1,256,5,4,128]{5,2,3,0,1,4:T(8,128)(2,1)}), bf16[2,1,256,5,4,128]{5,2,3,0,1,4:T(8,128)(2,1)}, u32[]{:S(2)}, u32[]{:S(2)}) async-start(bf16[2,1,256,5,4,128]{5,2,3,0,1,4:T(8,128)(2,1)} %copy.83), calls=%async_computation.1 | async-start | bytes 5242880 | tf_op jit(solution)/shard_map/all_to_all | solution.py:134
  568.9 25.0 %copy-start.1 = (bf16[1,5,128,2560]{3,2,1,0:T(8,128)(2,1)S(1)}, bf16[1,5,128,2560]{3,2,1,0:T(8,128)(2,1)}, u32[]{:S(2)}) copy-start(bf16[1,5,128,2560]{3,2,1,0:T(8,128)(2,1)} %param.19) | copy-start | bytes 9830404
where the time goes:
time: 604 us; the launch traced here: 594 us
  blocking collectives  370 us (61%)
  matrix products  107 us (18%)
  local copies, waits for them, and re-layouts  47.7 us (8%)
  other arithmetic  41.4 us (7%)
  starting transfers between devices  13.4 us (2%)
  waiting for transfers between devices  13.2 us (2%)
    psum x1, blocking collectives, run_prefill(): hidden = add_residual(hidden, lax.psum(part_sum, 'tp').astype(jnp.bfloat16))  188 us
    psum x1, blocking collectives, run_prefill(): hidden = add_residual(hidden, lax.psum(mlp_part, 'tp').astype(jnp.bfloat16))  182 us
    dot_general x2, matrix products, swiglu(): jnp.einsum('...d,kfd->...kf', normed, w_gu, preferred_element_type=jnp.fl...  34.3 us
    dot_general x2, matrix products, swiglu(): jnp.einsum('...f,fd->...d', activated, w_down, preferred_element_type=jnp...  21.1 us
    sub x1, matrix products, prompt_attention(): prob_bf = jax.nn.softmax(scores, axis=-1).astype(jnp.bfloat16)  14 us
    squeeze x1, local copies, waits for them, and re-layouts, run_prefill(): w_qkv[layer_idx]  13.9 us
    all_to_all x1, waiting for transfers between devices, rows_to_heads(): spread = lax.all_to_all(grouped, 'tp', 3, 1)  13.2 us
    unnamed x1, matrix products  13.2 us
  transfers between devices with their start and end apart: 3, of which 1 were waited for; matrix products, arithmetic and copies ran while one was open for 20% of the time, Pallas kernels for 0%

commit v1 on v0

v1 whole, which is shorter than its diff:
```python
import functools

import jax
import jax.numpy as jnp
from jax import lax
from jax.experimental import pallas as pl
from jax.experimental.pallas import tpu as pltpu
from jax.sharding import PartitionSpec as P

EPSILON = 1e-6
THETA = 10000.0
MASKED = -1e30
VMEM_LIMIT = 60 * 1024 * 1024
ANY = pl.BlockSpec(memory_space=pl.ANY)
VM = pl.BlockSpec(memory_space=pltpu.VMEM)
SM = pl.BlockSpec(memory_space=pltpu.SMEM)


def rms_norm(hidden, gain_vec):
    hid_f32 = hidden.astype(jnp.float32)
    inv_rms = lax.rsqrt(jnp.mean(hid_f32 * hid_f32, axis=-1, keepdims=True) + EPSILON)
    return (hid_f32 * inv_rms * gain_vec).astype(jnp.bfloat16)


def add_residual(hidden, update):
    return (hidden.astype(jnp.float32) + update.astype(jnp.float32)).astype(jnp.bfloat16)


def rope_tables(positions, head_dim):
    half_dim = head_dim // 2
    inv_freq = THETA ** (-jnp.arange(half_dim, dtype=jnp.float32) * 2.0 / head_dim)
    angles = positions.astype(jnp.float32)[:, None] * inv_freq[None, :]
    return jnp.cos(angles), jnp.sin(angles)


def apply_rope(values_in, cos_tab, sin_tab):
    half_dim = values_in.shape[-1] // 2
    lower_half = values_in[..., :half_dim]
    upper_half = values_in[..., half_dim:]
    cos_b = cos_tab[:, None, :]
    sin_b = sin_tab[:, None, :]
    return jnp.concatenate([lower_half * cos_b - upper_half * sin_b, upper_half * cos_b + lower_half * sin_b], axis=-1)


def front_kernel(len_ref, cos_ref, sin_ref, g1_ref, g2_ref, x_hbm, wqkv_hbm, wo_hbm, h_hbm, n_hbm, k_ref, v_ref, xs, ns, nv, wv, acc, qv, ctx, wo, wsem, xsem, osem, hsem, nsem, ssem, rsem, *, rb, tp_size, side_size):
    n_kind, heads, depth, head_dim = wqkv_hbm.shape
    rows = x_hbm.shape[0]
    n_blk = rows // rb
    shard = heads * head_dim
    width = n_kind * shard
    half = depth // 2
    me = lax.axis_index('tp')
    side = lax.axis_index('side')
    core = lax.rem(side, 2)
    chip = side // 2
    n_chip = side_size // 2
    part = shard // side_size
    tp_of = lambda d: lax.rem(me + d + tp_size, tp_size)
    chip_of = lambda d: lax.rem(chip + d + n_chip, n_chip)
    to_right = {'tp': tp_of(1)}
    to_left = {'tp': tp_of(-1)}
    to_up = {'side': chip_of(1) * 2 + core}
    to_down = {'side': chip_of(-1) * 2 + core}
    to_twin = {'side': chip * 2 + 1 - core}
    whole = pl.ds(0, depth)
    cols_a = pl.ds(0, half)
    cols_b = pl.ds(half, half)

    def send(idx, ref, dev, src=None):
        return pltpu.make_async_remote_copy(src_ref=ref if src is None else src, dst_ref=ref, send_sem=ssem.at[idx], recv_sem=rsem.at[idx], device_id=dev, device_id_type=pl.DeviceIdType.MESH)

    def w_part(d_tp, d_chip, cols, core_id):
        row0 = pl.multiple_of((chip_of(d_chip) * 2 + core_id) * part, 16)
        return wo.at[tp_of(d_tp), pl.ds(row0, part), cols]

    def c_part(d_tp, blk):
        return ctx.at[pl.ds(blk * rb, rb), pl.ds(pl.multiple_of(tp_of(d_tp) * shard, 128), shard)]

    offs = (-1, 1, 2)
    hops = (0, -1, 1, 2)
    sent = []

    def start(copy):
        copy.start()
        sent.append(copy)

    own_slice = wo_hbm.at[pl.ds(pl.multiple_of(side * part, 16), part), :]
    y_send = [
        lambda: send(0, w_part(0, 0, whole, core), to_right, src=own_slice),
        lambda: send(1, w_part(0, 0, whole, core), to_left, src=own_slice),
        lambda: send(2, w_part(-1, 0, cols_a, core), to_right),
        lambda: send(3, w_part(1, 0, cols_b, core), to_left),
    ]
    y_land = [
        lambda: send(0, w_part(-1, 0, whole, core), to_right),
        lambda: send(1, w_part(1, 0, whole, core), to_left),
        lambda: send(2, w_part(-2, 0, cols_a, core), to_right),
        lambda: send(3, w_part(2, 0, cols_b, core), to_left),
    ]

    def x_send(i, kind):
        d = offs[i]
        idx = 4 + 4 * i + kind
        if kind == 0:
            return send(idx, w_part(d, 0, whole, core), to_up)
        if kind == 1:
            return send(idx, w_part(d, 0, whole, core), to_down)
        if kind == 2:
            return send(idx, w_part(d, -1, cols_a, core), to_up)
        return send(idx, w_part(d, 1, cols_b, core), to_down)

    def x_land(i, kind):
        d = offs[i]
        idx = 4 + 4 * i + kind
        if kind == 0:
            return send(idx, w_part(d, -1, whole, core), to_up)
        if kind == 1:
            return send(idx, w_part(d, 1, whole, core), to_down)
        if kind == 2:
            return send(idx, w_part(d, -2, cols_a, core), to_up)
        return send(idx, w_part(d, 2, cols_b, core), to_down)

    def t_send(i, j):
        return send(16 + 4 * i + j, w_part(offs[i], hops[j], whole, core), to_twin)

    def t_land(i, j):
        return send(16 + 4 * i + j, w_part(offs[i], hops[j], whole, 1 - core), to_twin)

    c_right = lambda blk: send(28 + blk, c_part(0, blk), to_right)
    c_left = lambda blk: send(28 + n_blk + blk, c_part(0, blk), to_left)
    c_from_left = lambda blk: send(28 + blk, c_part(-1, blk), to_right)
    c_from_right = lambda blk: send(28 + n_blk + blk, c_part(1, blk), to_left)

    def f_send(blk):
        if blk < n_blk // 2:
            return send(28 + 2 * n_blk + blk, c_part(-1, blk), to_right)
        return send(28 + 2 * n_blk + blk, c_part(1, blk), to_left)

    def f_land(blk):
        return send(28 + 2 * n_blk + blk, c_part(2, blk), to_right if blk < n_blk // 2 else to_left)

    def w_copy(kind, head):
        idx = kind * heads + head
        return pltpu.make_async_copy(wqkv_hbm.at[kind, head], wv.at[:, pl.ds(idx * head_dim, head_dim)], wsem.at[idx])

    x_in = lambda blk: pltpu.make_async_copy(x_hbm.at[pl.ds(blk * rb, rb), :], nv.at[pl.ds(blk * rb, rb), :], xsem.at[blk])
    x_again = lambda blk: pltpu.make_async_copy(x_hbm.at[pl.ds(blk * rb, rb), :], xs.at[blk % 2], xsem.at[n_blk + blk])
    own_w = pltpu.make_async_copy(wo_hbm, wo.at[me], osem.at[0])

    for blk in range(n_blk):
        x_in(blk).start()
    for kind in range(n_kind):
        for head in range(heads):
            w_copy(kind, head).start()
    own_w.start()
    x_again(0).start()
    x_again(1).start()

    barrier = pltpu.get_barrier_semaphore()
    for dev in (to_right, to_left, to_up, to_down, to_twin):
        pl.semaphore_signal(barrier, inc=1, device_id=dev, device_id_type=pl.DeviceIdType.MESH)
    pl.semaphore_wait(barrier, 5)
    start(y_send[0]())
    start(y_send[1]())

    nb = 64
    for blk in range(n_blk):
        x_in(blk).wait()

    def norm_step(i, carry):
        r = pl.ds(pl.multiple_of(i * nb, nb), nb)
        nv[r, :] = rms_norm(nv[r, :], g1_ref[...])
        return carry

    lax.fori_loop(0, rows // nb, norm_step, 0)
    for kind in range(n_kind):
        for head in range(heads):
            w_copy(kind, head).wait()

    def qkv_step(i, carry):
        r = pl.ds(pl.multiple_of(i * rb, rb), rb)
        acc[pl.ds(0, rb), pl.ds(0, width)] = jnp.dot(nv[r, :], wv[...], preferred_element_type=jnp.float32)
        cos_b = cos_ref[r, :]
        sin_b = sin_ref[r, :]
        for head in range(heads):
            for kind, out in ((0, qv), (1, k_ref)):
                idx = (kind * heads + head) * head_dim
                val = acc[0:rb, idx:idx + head_dim]
                out[head, r, :] = (val * cos_b + pltpu.roll(val, head_dim // 2, 1) * sin_b).astype(jnp.bfloat16)
            idx = (2 * heads + head) * head_dim
            v_ref[head, r, :] = acc[0:rb, idx:idx + head_dim].astype(jnp.bfloat16)
        return carry

    lax.fori_loop(0, n_blk // 2, qkv_step, 0)
    for m in range(2):
        y_land[m]().wait_recv()
    for m in range(2):
        start(y_send[2 + m]())
    for i in range(2):
        start(x_send(i, 0))
        start(x_send(i, 1))
        start(t_send(i, 0))
    lax.fori_loop(n_blk // 2, n_blk, qkv_step, 0)
    for m in range(2):
        y_land[2 + m]().wait_recv()
    start(x_send(2, 0))
    start(x_send(2, 1))
    start(t_send(2, 0))

    valid = len_ref[0]
    scale = head_dim ** -0.5
    for blk in range(n_blk):
        span = (blk + 1) * rb
        rowi = lax.broadcasted_iota(jnp.int32, (rb, span), 0) + blk * rb
        coli = lax.broadcasted_iota(jnp.int32, (rb, span), 1)
        seen = (coli <= rowi) & (coli < valid)

        def head_step(head, carry, blk=blk, span=span, seen=seen):
            kk = k_ref[head, pl.ds(0, span), :]
            s = lax.dot_general(qv[head, pl.ds(blk * rb, rb), :], kk, (((1,), (1,)), ((), ())), preferred_element_type=jnp.float32)
            s = jnp.where(seen, s * scale, MASKED)
            p = jnp.exp(s - jnp.max(s, axis=-1, keepdims=True))
            p = (p * (1.0 / jnp.sum(p, axis=-1, keepdims=True))).astype(jnp.bfloat16)
            c = jnp.dot(p, v_ref[head, pl.ds(0, span), :], preferred_element_type=jnp.float32).astype(jnp.bfloat16)
            ctx[pl.ds(blk * rb, rb), pl.ds(pl.multiple_of(me * shard + head * head_dim, head_dim), head_dim)] = c
            return carry

        lax.fori_loop(0, heads, head_step, 0)
        start(c_right(blk))
        start(c_left(blk))

    def relay_x(i):
        for kind in range(2):
            x_land(i, kind).wait_recv()
        for kind in range(2):
            start(x_send(i, 2 + kind))
        start(t_send(i, 1))
        start(t_send(i, 2))

    relay_x(0)
    relay_x(1)
    own_w.wait()

    def add_shard(d, first):
        w_ref = wo.at[tp_of(d)]
        col = pl.ds(pl.multiple_of(tp_of(d) * shard, 128), shard)

        def step(i, carry):
            r = pl.ds(pl.multiple_of(i * rb, rb), rb)
            val = jnp.dot(ctx[r, col], w_ref[...], preferred_element_type=jnp.float32)
            if first:
                acc[r, :] = val
            else:
                acc[r, :] += val
            return carry

        lax.fori_loop(0, n_blk, step, 0)

    for blk in range(n_blk // 2):
        c_from_left(blk).wait_recv()
        start(f_send(blk))
    for blk in range(n_blk // 2, n_blk):
        c_from_right(blk).wait_recv()
        start(f_send(blk))
    add_shard(0, True)
    relay_x(2)
    for i in range(3):
        for kind in range(2, 4):
            x_land(i, kind).wait_recv()
        start(t_send(i, 3))
    for i in range(3):
        for j in range(4):
            t_land(i, j).wait_recv()
    for blk in range(n_blk // 2, n_blk):
        c_from_left(blk).wait_recv()
    for blk in range(n_blk // 2):
        c_from_right(blk).wait_recv()
    add_shard(-1, False)
    add_shard(1, False)

    col = pl.ds(pl.multiple_of(tp_of(2) * shard, 128), shard)
    h_copy = lambda blk: pltpu.make_async_copy(nv.at[pl.ds(blk * rb, rb), :], h_hbm.at[pl.ds(blk * rb, rb), :], hsem.at[blk])
    n_copy = lambda blk: pltpu.make_async_copy(ns.at[blk % 2], n_hbm.at[pl.ds(blk * rb, rb), :], nsem.at[blk])
    w_far = wo.at[tp_of(2)]
    for blk in range(n_blk):
        f_land(blk).wait_recv()
        x_again(blk).wait()
        if blk >= 2:
            n_copy(blk - 2).wait()
        r = pl.ds(blk * rb, rb)
        acc[r, :] += jnp.dot(ctx[r, col], w_far[...], preferred_element_type=jnp.float32)

        def end_step(i, carry, blk=blk):
            r = pl.ds(pl.multiple_of(blk * rb + i * nb, nb), nb)
            q = pl.ds(pl.multiple_of(i * nb, nb), nb)
            h = add_residual(xs[blk % 2, q, :], acc[r, :].astype(jnp.bfloat16))
            nv[r, :] = h
            ns[blk % 2, q, :] = rms_norm(h, g2_ref[...])
            return carry

        lax.fori_loop(0, rb // nb, end_step, 0)
        h_copy(blk).start()
        n_copy(blk).start()
        if blk + 2 < n_blk:
            x_again(blk + 2).start()
    for blk in range(n_blk):
        h_copy(blk).wait()
        if blk >= n_blk - 2:
            n_copy(blk).wait()
    for copy in sent:
        copy.wait_send()


def front_call(x, s_len, gain1, gain2, cos_full, sin_full, w_qkv, w_o, tp_size, side_size):
    rows, depth = x.shape
    n_kind, heads, _, head_dim = w_qkv.shape
    shard = heads * head_dim
    width = n_kind * shard
    rb = 256
    n_blk = rows // rb
    n_msg = 28 + 3 * n_blk
    act = jax.ShapeDtypeStruct((rows, depth), jnp.bfloat16)
    kv = jax.ShapeDtypeStruct((heads, rows, head_dim), jnp.bfloat16)
    dma = pltpu.SemaphoreType.DMA
    return pl.pallas_call(
        functools.partial(front_kernel, rb=rb, tp_size=tp_size, side_size=side_size),
        out_shape=(act, act, kv, kv),
        in_specs=[SM, VM, VM, VM, VM, ANY, ANY, ANY],
        out_specs=(ANY, ANY, VM, VM),
        scratch_shapes=[
            pltpu.VMEM((2, rb, depth), jnp.bfloat16),
            pltpu.VMEM((2, rb, depth), jnp.bfloat16),
            pltpu.VMEM((rows, depth), jnp.bfloat16),
            pltpu.VMEM((depth, width), jnp.bfloat16),
            pltpu.VMEM((rows, depth), jnp.float32),
            pltpu.VMEM((heads, rows, head_dim), jnp.bfloat16),
            pltpu.VMEM((rows, tp_size * shard), jnp.bfloat16),
            pltpu.VMEM((tp_size, shard, depth), jnp.bfloat16),
            dma((n_kind * heads,)), dma((2 * n_blk,)), dma((1,)), dma((n_blk,)), dma((n_blk,)), dma((n_msg,)), dma((n_msg,)),
        ],
        compiler_params=pltpu.CompilerParams(vmem_limit_bytes=67043328, collective_id=0, has_side_effects=True),
        cost_estimate=pl.CostEstimate(flops=2 * rows * depth * (width + tp_size * shard), bytes_accessed=2 * (4 * rows * depth + depth * width), transcendentals=0),
        name="front",
    )(s_len, cos_full, sin_full, gain1, gain2, x, w_qkv, w_o)


def mlp_kernel(idx_ref, n_hbm, wgu_hbm, wd_hbm, o0, o1, o2, o3, nv, gu_v, wd_v, acc, nsem, gsem, dsem, *, fb):
    ff, depth = wd_hbm.shape
    chunk = o0.shape[0]
    pieces = [(f, min(fb, ff - f)) for f in range(0, ff, fb)]

    def n_copy(c):
        src = n_hbm.at[pl.ds(pl.multiple_of(idx_ref[c] * chunk, chunk), chunk), :]
        return pltpu.make_async_copy(src, nv.at[pl.ds(c * chunk, chunk), :], nsem.at[c])

    def gu_copy(p, which):
        f, size = pieces[p]
        return pltpu.make_async_copy(wgu_hbm.at[which, pl.ds(f, size), :], gu_v.at[which, pl.ds(f, size), :], gsem.at[2 * p + which])

    def wd_copy(p):
        f, size = pieces[p]
        return pltpu.make_async_copy(wd_hbm.at[pl.ds(f, size), :], wd_v.at[pl.ds(f, size), :], dsem.at[p])

    n_copy(0).start()
    n_copy(1).start()
    for p in range(len(pieces)):
        gu_copy(p, 0).start()
        gu_copy(p, 1).start()
    for p in range(len(pieces)):
        wd_copy(p).start()
    n_copy(0).wait()
    n_copy(1).wait()
    nt = (((1,), (1,)), ((), ()))
    for p, (f, size) in enumerate(pieces):
        gu_copy(p, 0).wait()
        gu_copy(p, 1).wait()
        gate = lax.dot_general(nv[...], gu_v[0, f:f + size, :], nt, preferred_element_type=jnp.float32)
        up = lax.dot_general(nv[...], gu_v[1, f:f + size, :], nt, preferred_element_type=jnp.float32)
        gate = gate.astype(jnp.bfloat16).astype(jnp.float32)
        up = up.astype(jnp.bfloat16).astype(jnp.float32)
        acc[:, f:f + size] = (gate * jax.nn.sigmoid(gate) * up).astype(jnp.bfloat16)
    for p in range(len(pieces)):
        wd_copy(p).wait()
    half = depth // 2
    for lo, top, low in ((0, o0, o2), (half, o1, o3)):
        for c in range(0, half, fb):
            part = jnp.dot(acc[...], wd_v[:, lo + c:lo + c + fb], preferred_element_type=jnp.float32)
            top[:, c:c + fb] = part[:chunk]
            low[:, c:c + fb] = part[chunk:]


def mlp_call(idx, normed, w_gu, w_down, chunk):
    ff, depth = w_down.shape
    fb = 256
    n_piece = -(-ff // fb)
    out = jax.ShapeDtypeStruct((chunk, depth // 2), jnp.float32)
    return pl.pallas_call(
        functools.partial(mlp_kernel, fb=fb),
        out_shape=(out,) * 4,
        in_specs=[SM, ANY, ANY, ANY],
        out_specs=(VM,) * 4,
        scratch_shapes=[
            pltpu.VMEM((2 * chunk, depth), jnp.bfloat16),
            pltpu.VMEM((2, ff, depth), jnp.bfloat16),
            pltpu.VMEM((ff, depth), jnp.bfloat16),
            pltpu.VMEM((2 * chunk, ff), jnp.bfloat16),
            pltpu.SemaphoreType.DMA((2,)),
            pltpu.SemaphoreType.DMA((2 * n_piece,)),
            pltpu.SemaphoreType.DMA((n_piece,)),
        ],
        compiler_params=pltpu.CompilerParams(vmem_limit_bytes=VMEM_LIMIT),
        cost_estimate=pl.CostEstimate(flops=12 * chunk * ff * depth, bytes_accessed=6 * ff * depth + 12 * chunk * depth, transcendentals=0),
        name="mlp",
    )(idx, normed, w_gu, w_down)


def assemble_kernel(own, left, right, top, low, out, sems, *, tp_size):
    rows = own.shape[0]
    half = rows // 2
    me = lax.axis_index('tp')
    spot = lambda d, off: pl.multiple_of(lax.rem(me + d + tp_size, tp_size) * rows + off, half)
    places = ((own, 0, 0, rows), (left, -1, 0, rows), (right, 1, 0, rows), (top, 2, 0, half), (low, 2, half, half))
    copies = [pltpu.make_async_copy(ref, out.at[pl.ds(spot(d, off), size), :], sems.at[n]) for n, (ref, d, off, size) in enumerate(places)]
    for copy in copies:
        copy.start()
    for copy in copies:
        copy.wait()


def assemble_call(own, left, right, top, low, tp_size):
    rows, width = own.shape
    return pl.pallas_call(
        functools.partial(assemble_kernel, tp_size=tp_size),
        out_shape=jax.ShapeDtypeStruct((tp_size * rows, width), own.dtype),
        in_specs=[VM] * 5,
        out_specs=ANY,
        scratch_shapes=[pltpu.SemaphoreType.DMA((5,))],
        compiler_params=pltpu.CompilerParams(vmem_limit_bytes=32 * 1024 * 1024),
        cost_estimate=pl.CostEstimate(flops=rows * width, bytes_accessed=16 * rows * width, transcendentals=0),
        name="assemble",
    )(own, left, right, top, low)


def ring_gather(block, right, left, me, tp_size):
    rows = block.shape[0]
    half = rows // 2
    from_left = lax.ppermute(block, 'tp', right)
    from_right = lax.ppermute(block, 'tp', left)
    far_top = lax.ppermute(from_left[:half], 'tp', right)
    far_low = lax.ppermute(from_right[half:], 'tp', left)
    return assemble_call(block, from_left, from_right, far_top, far_low, tp_size)


def move_kv(k, v, me, tp_size, side_size):
    heads = k.shape[0]
    kv = jnp.stack([k, v], axis=1)
    pieces = []
    for off in range(tp_size):
        group = list(range(off, heads, tp_size))
        perm = []
        for t in range(tp_size):
            for s in range(side_size):
                perm.append((t * side_size + s, (t + off) % tp_size * side_size + (s + side_size // 2) % side_size))
        got = lax.ppermute(jnp.stack([kv[i] for i in group]), ('tp', 'side'), perm)
        pieces.extend((group[n], got[n]) for n in range(len(group)))
    stacked = jnp.stack([piece for _, piece in sorted(pieces, key=lambda item: item[0])])
    head_ids = jnp.arange(heads) * tp_size + me
    picked = jnp.take(stacked, head_ids % heads, axis=0)
    return picked[:, 0], picked[:, 1]


def small_psum(part, tp_size):
    rows, width = part.shape
    blocks = lax.all_to_all(part.reshape(tp_size, rows // tp_size, width), 'tp', 0, 0)
    total = blocks[0]
    for i in range(1, tp_size):
        total = total + blocks[i]
    mine = jnp.broadcast_to(total.astype(jnp.bfloat16)[None], (tp_size, rows // tp_size, width))
    return lax.all_to_all(mine, 'tp', 0, 0).reshape(rows, width)


def swiglu(hidden, gain_vec, w_gu, w_down):
    normed = rms_norm(hidden, gain_vec)
    gate_up = jnp.einsum('...d,kfd->...kf', normed, w_gu, preferred_element_type=jnp.float32)
    gate_val = gate_up[..., 0, :].astype(jnp.bfloat16).astype(jnp.float32)
    up_val = gate_up[..., 1, :].astype(jnp.bfloat16).astype(jnp.float32)
    activated = (jax.nn.silu(gate_val) * up_val).astype(jnp.bfloat16)
    return jnp.einsum('...f,fd->...d', activated, w_down, preferred_element_type=jnp.float32)


def decode_attention(queries, k_tok, v_tok, k_layer, v_layer, visible):
    attn_scale = queries.shape[-1] ** -0.5
    cache_scores = jnp.einsum('bhe,bthe->bht', queries, k_layer, preferred_element_type=jnp.float32) * attn_scale
    cache_scores = jnp.where(visible, cache_scores, MASKED)
    self_score = jnp.einsum('bhe,bhe->bh', queries, k_tok, preferred_element_type=jnp.float32) * attn_scale
    row_max = jnp.maximum(jnp.max(cache_scores, axis=-1), self_score)
    cache_exp = jnp.exp(cache_scores - row_max[..., None])
    self_exp = jnp.exp(self_score - row_max)
    denominator = jnp.sum(cache_exp, axis=-1) + self_exp
    cache_prob = (cache_exp / denominator[..., None]).astype(jnp.bfloat16)
    self_prob = (self_exp / denominator).astype(jnp.bfloat16).astype(jnp.float32)
    context = jnp.einsum('bht,bthe->bhe', cache_prob, v_layer, preferred_element_type=jnp.float32) + self_prob[..., None] * v_tok.astype(jnp.float32)
    return context.astype(jnp.bfloat16)


def run_decode(tokens, k_cache, v_cache, c_len, w_qkv, w_out, w_gu, w_down, gains, tp_size):
    layers, row_count, cache_len, heads_loc, _, head_dim = k_cache.shape
    model_width = tokens.shape[1]
    k_local = k_cache.reshape(layers, row_count, cache_len, heads_loc, head_dim)
    v_local = v_cache.reshape(layers, row_count, cache_len, heads_loc, head_dim)
    wqkv_local = w_qkv.reshape(layers, model_width, 3, heads_loc, head_dim)
    wout_local = w_out.reshape(layers, heads_loc, head_dim, model_width)
    cos_tab, sin_tab = rope_tables(c_len, head_dim)
    cache_pos = jnp.arange(cache_len)
    visible = (cache_pos[None, :] < c_len[:, None])[:, None, :]
    write_at = (cache_pos[None, :] == c_len[:, None])[:, :, None, None]
    k_next = []
    v_next = []
    for layer_idx in range(layers):
        normed = rms_norm(tokens, gains[layer_idx, 0])
        qkv_out = jnp.einsum('bd,dkhe->bkhe', normed, wqkv_local[layer_idx], preferred_element_type=jnp.float32)
        queries = apply_rope(qkv_out[:, 0], cos_tab, sin_tab).astype(jnp.bfloat16)
        k_tok = apply_rope(qkv_out[:, 1], cos_tab, sin_tab).astype(jnp.bfloat16)
        v_tok = qkv_out[:, 2].astype(jnp.bfloat16)
        context = decode_attention(queries, k_tok, v_tok, k_local[layer_idx], v_local[layer_idx], visible)
        part_sum = jnp.einsum('bhe,hed->bd', context, wout_local[layer_idx], preferred_element_type=jnp.float32)
        tokens = add_residual(tokens, small_psum(part_sum, tp_size))
        mlp_part = swiglu(tokens, gains[layer_idx, 1], w_gu[layer_idx], w_down[layer_idx])
        tokens = add_residual(tokens, small_psum(mlp_part, tp_size))
        k_next.append(jnp.where(write_at, k_tok[:, None], k_local[layer_idx]))
        v_next.append(jnp.where(write_at, v_tok[:, None], v_local[layer_idx]))
    return tokens, jnp.stack(k_next).reshape(k_cache.shape), jnp.stack(v_next).reshape(v_cache.shape)


def run_prefill(prompt, s_len, w_qkv, w_out, w_gu, w_down, gains, tp_size, side_size):
    rows, width = prompt.shape
    layers, _, _, heads_loc, head_dim = w_qkv.shape
    me = lax.axis_index('tp')
    right = [(i, (i + 1) % tp_size) for i in range(tp_size)]
    left = [(i, (i - 1) % tp_size) for i in range(tp_size)]
    cos_tab, sin_tab = rope_tables(jnp.arange(rows), head_dim)
    cos_full = jnp.concatenate([cos_tab, cos_tab], axis=-1)
    sin_full = jnp.concatenate([-sin_tab, sin_tab], axis=-1)
    chunk = rows // tp_size
    half = width // 2
    ids = (me + jnp.array([-1, 1, 2, 0], jnp.int32)) % tp_size
    hidden = prompt
    kv_layers = []
    for layer in range(layers):
        shard = heads_loc * head_dim
        w_o = w_out[layer].reshape(shard, width)
        w_t = w_qkv[layer].transpose(1, 2, 0, 3)
        hidden, normed, k, v = front_call(hidden, s_len, gains[layer, 0][None], gains[layer, 1][None], cos_full, sin_full, w_t, w_o, tp_size, side_size)
        kv_layers.append(move_kv(k, v, me, tp_size, side_size))
        a = mlp_call(ids[:2], normed, w_gu[layer], w_down[layer], chunk)
        b = mlp_call(ids[2:], normed, w_gu[layer], w_down[layer], chunk)
        go_r = a[0]
        go_l = a[3]
        for own_r, own_l in ((b[0], b[1]), (a[2], a[1]), (b[2], b[3])):
            go_r = lax.ppermute(go_r, 'tp', right) + own_r
            go_l = lax.ppermute(go_l, 'tp', left) + own_l
        mine = lax.dynamic_slice_in_dim(hidden, me * chunk, chunk, 0)
        down = jnp.concatenate([go_r, go_l], axis=1).astype(jnp.bfloat16)
        hidden = ring_gather(add_residual(mine, down), right, left, me, tp_size)
    return hidden, kv_layers


def solution(mesh):
    tp_size = mesh.shape['tp']
    side_size = mesh.shape['side']
    inst_axes = ('pair', 'side')
    rows_spec = P(inst_axes, None)
    vec_spec = P(inst_axes)
    cache_spec = P(None, inst_axes, None, None, 'tp', None)
    prompt_spec = P(None, inst_axes, None, 'tp', None)
    in_specs = (rows_spec, vec_spec, P(None, None, None, 'tp', None), P(None, 'tp', None, None), P(None, None, 'tp', None), P(None, 'tp', None), P(None, None, None), rows_spec, cache_spec, cache_spec, vec_spec, P(None, None, None, None, 'tp', None), P(None, None, 'tp', None, None), P(None, None, 'tp', None), P(None, 'tp', None), P(None, None, None))
    out_specs = (rows_spec, rows_spec, prompt_spec, prompt_spec, cache_spec, cache_spec)

    def device_fn(prompt_x, s_len, w_qkv_pre, w_out_pre, w_gu_pre, w_down_pre, gain_pre, dec_tokens, k_cache, v_cache, c_len, w_qkv_dec, w_out_dec, w_gu_dec, w_down_dec, gain_dec):
        hidden, kv_layers = run_prefill(prompt_x, s_len, w_qkv_pre, w_out_pre, w_gu_pre, w_down_pre, gain_pre, tp_size, side_size)
        k_prompt = jnp.stack([k for k, _ in kv_layers]).transpose(0, 2, 1, 3)[:, :, :, None, :]
        v_prompt = jnp.stack([v for _, v in kv_layers]).transpose(0, 2, 1, 3)[:, :, :, None, :]
        dec_out, k_cache_new, v_cache_new = run_decode(dec_tokens, k_cache, v_cache, c_len, w_qkv_dec, w_out_dec, w_gu_dec, w_down_dec, gain_dec, tp_size)
        return hidden, dec_out, k_prompt, v_prompt, k_cache_new, v_cache_new

    return jax.shard_map(device_fn, mesh=mesh, in_specs=in_specs, out_specs=out_specs, check_vma=False)
```

time: 604 us -> 355 us (0.59)
  blocking collectives: 370 us -> 0 us
  Pallas kernels: 0 us -> 150 us
  matrix products: 107 us -> 30.1 us
  waiting for transfers between devices: 13.2 us -> 72.6 us
  starting transfers between devices: 13.4 us -> 43.3 us
  local copies, waits for them, and re-layouts: 47.7 us -> 19.2 us
  other arithmetic: 41.4 us -> 32.9 us
    psum x2 -> x0, blocking collectives: 370 us -> none  [the longest x1 188 us: run_prefill(): hidden = add_residual(hidden, lax.psum(part_sum, 'tp').astype(jnp.bfloat16))]
    pallas_call x0 -> x4, Pallas kernels: none -> 150 us  [the longest x1 90.7 us: front_call(): pl.pallas_call(functools.partial(front_kernel, rb=rb, tp_size=tp_size, si...]
    ppermute x1 -> x14, waiting for transfers between devices: 0.01 us -> 44.1 us  [the longest x3 15.2 us: run_prefill(): go_l = lax.ppermute(go_l, 'tp', left) + own_l]
    ppermute x1 -> x14, starting transfers between devices: 3.41 us -> 26.9 us  [the longest x4 10.3 us: move_kv(): got = lax.ppermute(jnp.stack([kv[i] for i in group]), ('tp', 'side'), perm)]
    dot_general x2 -> x1, matrix products: 34.3 us -> 10.8 us  [swiglu(): jnp.einsum('...d,kfd->...kf', normed, w_gu, preferred_element_type=jnp.fl...]
    squeeze x2 -> x0, local copies, waits for them, and re-layouts: 17 us -> none  [the longest x1 13.9 us: run_prefill(): w_qkv[layer_idx]]
    dot_general x2 -> x1, matrix products: 21.1 us -> 5.51 us  [swiglu(): jnp.einsum('...f,fd->...d', activated, w_down, preferred_element_type=jnp...]
    all_to_all x2 -> x4, waiting for transfers between devices: 13.2 us -> 28.5 us  [the longest x2 15.7 us: small_psum(): lax.all_to_all(part.reshape(tp_size, rows // tp_size, width), 'tp', 0, 0)]
  transfers between devices with their start and end apart: 3 -> 18, of which waited for: 1 -> 8; matrix products, arithmetic and copies ran while one was open for 20% -> 22% of each run, Pallas kernels for 0% -> 8%
where the time goes in v1:
time: 355 us; the launch traced here: 350 us
  Pallas kernels  150 us (42%)
  waiting for transfers between devices  72.6 us (20%)
  starting transfers between devices  43.3 us (12%)
  other arithmetic  32.9 us (9%)
  matrix products  30.1 us (8%)
  local copies, waits for them, and re-layouts  19.2 us (5%)
    pallas_call x1, Pallas kernels, front_call(): pl.pallas_call(functools.partial(front_kernel, rb=rb, tp_size=tp_size, si...  90.7 us
    pallas_call x2, Pallas kernels, mlp_call(): pl.pallas_call(functools.partial(mlp_kernel, fb=fb), out_shape=(out,) * 4...  55.9 us
    all_to_all x2, waiting for transfers between devices, small_psum(): lax.all_to_all(part.reshape(tp_size, rows // tp_size, width), 'tp', 0, 0)  15.7 us
    ppermute x3, waiting for transfers between devices, run_prefill(): go_l = lax.ppermute(go_l, 'tp', left) + own_l  15.2 us
    all_to_all x2, waiting for transfers between devices, small_psum(): return lax.all_to_all(mine, 'tp', 0, 0).reshape(rows, width)  12.8 us
    ppermute x1, waiting for transfers between devices, ring_gather(): from_left = lax.ppermute(block, 'tp', right)  12.6 us
    dot_general x1, matrix products, swiglu(): jnp.einsum('...d,kfd->...kf', normed, w_gu, preferred_element_type=jnp.fl...  10.8 us
    ppermute x4, starting transfers between devices, move_kv(): got = lax.ppermute(jnp.stack([kv[i] for i in group]), ('tp', 'side'), perm)  10.3 us
  transfers between devices with their start and end apart: 18, of which 8 were waited for; matrix products, arithmetic and copies ran while one was open for 22% of the time, Pallas kernels for 8%

profile of v1, /device:TPU:96, one launch (start us, length us, event | category | flops | bytes accessed | tf_op | source)
XLA Modules:
  0.0 350.3 jit_solution(6342053050321604701)
XLA Ops:
  7.2 90.7 %front.1 = (bf16[1024,2560]{1,0:T(8,128)(2,1)}, bf16[1024,2560]{1,0:T(8,128)(2,1)}, bf16[5,1024,128]{2,1,0:T(8,128)(2,1)}, bf16[5,1024,128]{2,1,0:T(8,128)(2,1)}) custom-call(s32[1]{0:T(128)S(6)} %copy.64.len_ref, f32[1024,128]{1,0:T(8,128)} %get-tuple-element.80.cos_ref, f32[1024,128]{1,0:T(8,128)} %get-tuple-element.81.sin_ref, ...), custom_call_target="tpu_custom_call" | custom-call | flops 23488102400 | bytes 30801920 | tf_op jit(solution)/shard_map/front/pallas_call | solution.py:325
  98.0 28.0 %mlp.2 = (f32[256,1280]{1,0:T(8,128)}, f32[256,1280]{1,0:T(8,128)}, f32[256,1280]{1,0:T(8,128)}, f32[256,1280]{1,0:T(8,128)}) custom-call(s32[2]{0:T(128)} %get-tuple-element.79.idx_ref, bf16[1024,2560]{1,0:T(8,128)(2,1)} %get-tuple-element.19.n_hbm, bf16[2,1728,2560]{2,1,0:T(8,128)(2,1)} %bitcast.106, bf16[1728,2560]{1,0:T(8,128)(2,1)} %bitcast.109), custom_call_target="tpu_custom_call" | custom-call | flops 13589544960 | bytes 34406400 | tf_op jit(solution)/shard_map/mlp/pallas_call | solution.py:397
  126.0 3.6 %collective-permute-start.3 = (f32[256,1280]{1,0:T(8,128)}, f32[256,1280]{1,0:T(8,128)}, u32[]{:S(2)}, u32[]{:S(2)}) collective-permute-start(f32[256,1280]{1,0:T(8,128)} %get-tuple-element.24), channel_id=1, source_target_pairs={{0,24},{8,0},{16,8},{24,16},{1,25},{9,1},{17,9},{25,17},{2,26},{10... | collective-permute-start | bytes 3932168 | tf_op jit(solution)/shard_map/ppermute | solution.py:561
  130.1 5.2 %fusion.2 = f32[16,3,5,128]{3,0,2,1:T(8,128)S(1)} fusion(bf16[1,2560,3,5,1,128]{5,1,4,3,2,0:T(8,128)(2,1)} %param.28, bf16[16,2560]{1,0:T(8,128)(2,1)S(1)} %copy-done.9, f32[2560]{0:T(1024)S(1)} %get-tuple-element.43, f32[16]{0:T(128)S(1)} %add_rsqrt_fusion.1), kind=kOutput, calls=%fused_computation.3 | convolution fusion | flops 157450240 | bytes 10045504 | tf_op jit(solution)/shard_map/bd,dkhe->bkhe/dot_general | solution.py:521
  135.9 3.9 %fusion.8 = f32[16,5,1,256]{3,2,1,0:T(1,128)S(1)} fusion(bf16[1,16,256,5,1,128]{5,2,4,3,1,0:T(8,128)(2,1)} %param.25, bf16[16,5,128,1]{2,0,1,3:T(8,128)(2,1)S(1)} %fusion.53), kind=kOutput, calls=%fused_computation.9 | convolution fusion | flops 5242880 | bytes 5345280 | tf_op jit(solution)/shard_map/bhe,bthe->bht/dot_general | solution.py:493
  140.2 3.4 fusion.6
  145.0 4.5 %all-to-all-start = ((f32[4,4,2560]{2,1,0:T(4,128)}), f32[4,4,2560]{2,1,0:T(4,128)S(1)}, u32[]{:S(2)}, u32[]{:S(2)}) async-start(f32[4,4,2560]{2,1,0:T(4,128)} %convolution_bitcast_fusion), calls=%async_computation | async-start | bytes 327680 | tf_op jit(solution)/shard_map/all_to_all | solution.py:474
  153.3 3.5 %collective-permute-start.11 = (bf16[1,2,1024,128]{3,2,0,1:T(8,128)(2,1)}, bf16[1,2,1024,128]{3,2,0,1:T(8,128)(2,1)}, u32[]{:S(2)}, u32[]{:S(2)}) collective-permute-start(bf16[1,2,1024,128]{3,2,0,1:T(8,128)(2,1)} %get-tuple-element.55), channel_id=1, source_target_pairs={{0,12},{1,13},{2,14},{3,15},{4,8},{5,9},{6,10},{7,11},{8,20},{9,21... | collective-permute-start | bytes 1572872 | tf_op jit(solution)/shard_map/ppermute | solution.py:464
  156.8 3.6 %collective-permute-start.12 = (bf16[1,2,1024,128]{3,2,0,1:T(8,128)(2,1)}, bf16[1,2,1024,128]{3,2,0,1:T(8,128)(2,1)}, u32[]{:S(2)}, u32[]{:S(2)}) collective-permute-start(bf16[1,2,1024,128]{3,2,0,1:T(8,128)(2,1)} %get-tuple-element.56), channel_id=1, source_target_pairs={{0,20},{1,21},{2,22},{3,23},{4,16},{5,17},{6,18},{7,19},{8,28},{9,... | collective-permute-start | bytes 1572872 | tf_op jit(solution)/shard_map/ppermute | solution.py:464
  160.4 27.8 %mlp.3 = (f32[256,1280]{1,0:T(8,128)}, f32[256,1280]{1,0:T(8,128)}, f32[256,1280]{1,0:T(8,128)}, f32[256,1280]{1,0:T(8,128)}) custom-call(s32[2]{0:T(128)} %get-tuple-element.78.idx_ref, bf16[1024,2560]{1,0:T(8,128)(2,1)} %get-tuple-element.19.n_hbm, bf16[2,1728,2560]{2,1,0:T(8,128)(2,1)} %bitcast.107, bf16[1728,2560]{1,0:T(8,128)(2,1)} %bitcast.110), custom_call_target="tpu_custom_call" | custom-call | flops 13589544960 | bytes 34406400 | tf_op jit(solution)/shard_map/mlp/pallas_call | solution.py:397
  189.0 3.4 all-to-all-start.1
  192.4 9.1 %broadcast_select_fusion = (bf16[1,16,256,5,1,128]{5,2,4,3,1,0:T(8,128)(2,1)}, bf16[1,16,256,5,1,128]{5,2,4,3,1,0:T(8,128)(2,1)}) fusion(bf16[1,16,256,5,1,128]{5,2,4,3,1,0:T(8,128)(2,1)} %param.26, pred[16,256]{1,0:T(8,128)(4,1)S(1)} %get-tuple-element.76, bf16[16,5,128]{2,1,0:T(8,128)(2,1)S(1)} %copy.32, bf16[1,16,256,5,1,128]{5,2,4,3,1,0:T(8,128)(2,1)} %param.25, ...), kind=kLoop, calls=%fused_computation.11 | loop fusion | flops 5242880 | bytes 21016576 | tf_op jit(solution)/shard_map/jit(_where)/select_n | solution.py:531
  212.3 10.8 %fusion.11 = bf16[16,2,1728]{2,0,1:T(8,128)(2,1)S(1)} fusion(bf16[1,2,1728,2560]{3,2,1,0:T(8,128)(2,1)} %param.30, bf16[16,2560]{1,0:T(8,128)(2,1)S(1)} %get-tuple-element.45, f32[2560]{0:T(1024)S(1)} %get-tuple-element.42, f32[16]{0:T(128)S(1)} %add_rsqrt_fusion), kind=kOutput, calls=%fused_computation.25 | convolution fusion | flops 283334656 | bytes 17897536 | tf_op jit(solution)/shard_map/...d,kfd->...kf/dot_general | solution.py:484
  223.2 15.2 %collective-permute-done.4 = f32[256,1280]{1,0:T(8,128)S(1)} collective-permute-done((f32[256,1280]{1,0:T(8,128)}, f32[256,1280]{1,0:T(8,128)S(1)}, u32[]{:S(2)}, u32[]{:S(2)}) %collective-permute-start.4) | collective-permute-done | bytes 1310752 | tf_op jit(solution)/shard_map/ppermute | solution.py:561
  241.9 5.5 %fusion.4 = f32[4,4,2560]{2,1,0:T(4,128)} fusion(bf16[4,4,1728]{2,1,0:T(4,128)(2,1)S(1)} %convert_element_type.141, bf16[1,1728,2560]{2,1,0:T(8,128)(2,1)} %param.31), kind=kOutput, calls=%fused_computation.5 | convolution fusion | flops 141557760 | bytes 9066496 | tf_op jit(solution)/shard_map/...f,fd->...d/dot_general | solution.py:488
  247.4 3.6 %all-to-all-start.2 = ((f32[4,4,2560]{2,1,0:T(4,128)}), f32[4,4,2560]{2,1,0:T(4,128)S(1)}, u32[]{:S(2)}, u32[]{:S(2)}) async-start(f32[4,4,2560]{2,1,0:T(4,128)} %fusion.4), calls=%async_computation.2 | async-start | bytes 327680 | tf_op jit(solution)/shard_map/all_to_all | solution.py:474
  255.5 15.7 %all-to-all-done.2 = f32[4,4,2560]{2,1,0:T(4,128)S(1)} async-done(((f32[4,4,2560]{2,1,0:T(4,128)}), f32[4,4,2560]{2,1,0:T(4,128)S(1)}, u32[]{:S(2)}, u32[]{:S(2)}) %all-to-all-start.2) | async-done | bytes 163872 | tf_op jit(solution)/shard_map/all_to_all | solution.py:474
  271.9 5.0 %all-to-all-start.3 = ((bf16[4,4,2560]{2,1,0:T(4,128)(2,1)}), bf16[4,4,2560]{2,1,0:T(4,128)(2,1)S(1)}, u32[]{:S(2)}, u32[]{:S(2)}) async-start(bf16[4,4,2560]{2,1,0:T(4,128)(2,1)} %broadcast_in_dim.94), calls=%async_computation.3 | async-start | bytes 163840 | tf_op jit(solution)/shard_map/all_to_all | solution.py:479
  276.9 9.6 %all-to-all-done.3 = bf16[4,4,2560]{2,1,0:T(4,128)(2,1)S(1)} async-done(((bf16[4,4,2560]{2,1,0:T(4,128)(2,1)}), bf16[4,4,2560]{2,1,0:T(4,128)(2,1)S(1)}, u32[]{:S(2)}, u32[]{:S(2)}) %all-to-all-start.3) | async-done | bytes 81952 | tf_op jit(solution)/shard_map/all_to_all | solution.py:479
  305.4 4.3 %gather_fusion = bf16[5,2,1024,128]{3,2,1,0:T(8,128)(2,1)} fusion(bf16[5,2,1024,128]{3,2,0,1:T(8,128)(2,1)} %slice_dynamic-update-slice_fusion, s32[1024]{0:T(1024)S(1)} %pad_clamp_fusion), kind=kCustom, calls=%fused_computation | custom fusion | bytes 5242900 | tf_op jit(solution)/shard_map/jit(_take)/gather | solution.py:468
  309.7 12.6 %collective-permute-done.6.left = bf16[256,2560]{1,0:T(8,128)(2,1)S(1)} collective-permute-done((bf16[256,2560]{1,0:T(8,128)(2,1)S(1)}, bf16[256,2560]{1,0:T(8,128)(2,1)S(1)}, u32[]{:S(2)}, u32[]{:S(2)}) %collective-permute-start.6) | collective-permute-done | bytes 1310752 | tf_op jit(solution)/shard_map/ppermute | solution.py:447
  323.5 4.9 %collective-permute-done.7.right = bf16[256,2560]{1,0:T(8,128)(2,1)} collective-permute-done((bf16[256,2560]{1,0:T(8,128)(2,1)S(1)}, bf16[256,2560]{1,0:T(8,128)(2,1)}, u32[]{:S(2)}, u32[]{:S(2)}) %collective-permute-start.7) | collective-permute-done | bytes 1310752 | tf_op jit(solution)/shard_map/ppermute | solution.py:448
  336.9 9.5 %collective-permute-done.9.low = bf16[128,2560]{1,0:T(8,128)(2,1)S(1)} collective-permute-done((bf16[128,2560]{1,0:T(8,128)(2,1)S(1)}, bf16[128,2560]{1,0:T(8,128)(2,1)S(1)}, u32[]{:S(2)}, u32[]{:S(2)}) %collective-permute-start.9) | collective-permute-done | bytes 655392 | tf_op jit(solution)/shard_map/ppermute | solution.py:450
  346.4 3.7 %assemble.1 = bf16[1024,2560]{1,0:T(8,128)(2,1)} custom-call(bf16[256,2560]{1,0:T(8,128)(2,1)S(1)} %add_convert_fusion.own, bf16[256,2560]{1,0:T(8,128)(2,1)S(1)} %collective-permute-done.6.left, bf16[256,2560]{1,0:T(8,128)(2,1)} %collective-permute-done.7.right, bf16[128,2560]{1,0:T(8,128)(2,1)S(1)} %collective-permute-done.8.top, ...), custom_call_target="tpu_custom_call" | custom-call | flops 655360 | bytes 10485760 | tf_op jit(solution)/shard_map/assemble/pallas_call | solution.py:432
  (109 shorter events, 61.2 us)
Async XLA Ops:
  97.9 31.9 %copy-start.13 = (s32[16]{0:T(128)S(1)}, s32[16]{0:T(128)}, u32[]{:S(2)}) copy-start(s32[16]{0:T(128)} %param.27) | copy-start | bytes 196
  97.9 32.0 %copy-start.10 = (f32[1,2,2560]{2,1,0:T(2,128)S(1)}, f32[1,2,2560]{2,1,0:T(2,128)}, u32[]{:S(2)}) copy-start(f32[1,2,2560]{2,1,0:T(2,128)} %param.32) | copy-start | bytes 61444
  97.9 32.0 %copy-start.9 = (bf16[16,2560]{1,0:T(8,128)(2,1)S(1)}, bf16[16,2560]{1,0:T(8,128)(2,1)}, u32[]{:S(2)}) copy-start(bf16[16,2560]{1,0:T(8,128)(2,1)} %param.24) | copy-start | bytes 245764
  126.0 78.9 %collective-permute-start.3 = (f32[256,1280]{1,0:T(8,128)}, f32[256,1280]{1,0:T(8,128)}, u32[]{:S(2)}, u32[]{:S(2)}) collective-permute-start(f32[256,1280]{1,0:T(8,128)} %get-tuple-element.24), channel_id=1, source_target_pairs={{0,24},{8,0},{16,8},{24,16},{1,25},{9,1},{17,9},{25,17},{2,26},{10... | collective-permute-start | bytes 3932168 | tf_op jit(solution)/shard_map/ppermute | solution.py:561
  129.6 79.0 %collective-permute-start = (f32[256,1280]{1,0:T(8,128)}, f32[256,1280]{1,0:T(8,128)}, u32[]{:S(2)}, u32[]{:S(2)}) collective-permute-start(f32[256,1280]{1,0:T(8,128)} %get-tuple-element.20), channel_id=1, source_target_pairs={{0,8},{8,16},{16,24},{24,0},{1,9},{9,17},{17,25},{25,1},{2,10},{10... | collective-permute-start | bytes 3932168 | tf_op jit(solution)/shard_map/ppermute | solution.py:560
  145.0 43.3 %all-to-all-start = ((f32[4,4,2560]{2,1,0:T(4,128)}), f32[4,4,2560]{2,1,0:T(4,128)S(1)}, u32[]{:S(2)}, u32[]{:S(2)}) async-start(f32[4,4,2560]{2,1,0:T(4,128)} %convolution_bitcast_fusion), calls=%async_computation | async-start | bytes 327680 | tf_op jit(solution)/shard_map/all_to_all | solution.py:474
  151.8 142.8 %collective-permute-start.10 = (bf16[2,2,1024,128]{3,2,0,1:T(8,128)(2,1)}, bf16[2,2,1024,128]{3,2,0,1:T(8,128)(2,1)}, u32[]{:S(2)}, u32[]{:S(2)}) collective-permute-start(bf16[2,2,1024,128]{3,2,0,1:T(8,128)(2,1)} %pad_maximum_fusion), channel_id=1, source_target_pairs={{0,4},{1,5},{2,6},{3,7},{4,0},{5,1},{6,2},{7,3},{8,12},{9,13},{10,... | collective-permute-start | bytes 3145736 | tf_op jit(solution)/shard_map/ppermute | solution.py:464
  153.3 145.5 %collective-permute-start.11 = (bf16[1,2,1024,128]{3,2,0,1:T(8,128)(2,1)}, bf16[1,2,1024,128]{3,2,0,1:T(8,128)(2,1)}, u32[]{:S(2)}, u32[]{:S(2)}) collective-permute-start(bf16[1,2,1024,128]{3,2,0,1:T(8,128)(2,1)} %get-tuple-element.55), channel_id=1, source_target_pairs={{0,12},{1,13},{2,14},{3,15},{4,8},{5,9},{6,10},{7,11},{8,20},{9,21... | collective-permute-start | bytes 1572872 | tf_op jit(solution)/shard_map/ppermute | solution.py:464
  156.8 143.9 %collective-permute-start.12 = (bf16[1,2,1024,128]{3,2,0,1:T(8,128)(2,1)}, bf16[1,2,1024,128]{3,2,0,1:T(8,128)(2,1)}, u32[]{:S(2)}, u32[]{:S(2)}) collective-permute-start(bf16[1,2,1024,128]{3,2,0,1:T(8,128)(2,1)} %get-tuple-element.56), channel_id=1, source_target_pairs={{0,20},{1,21},{2,22},{3,23},{4,16},{5,17},{6,18},{7,19},{8,28},{9,... | collective-permute-start | bytes 1572872 | tf_op jit(solution)/shard_map/ppermute | solution.py:464
  189.0 15.7 %all-to-all-start.1 = ((bf16[4,4,2560]{2,1,0:T(4,128)(2,1)}), bf16[4,4,2560]{2,1,0:T(4,128)(2,1)S(1)}, u32[]{:S(2)}, u32[]{:S(2)}) async-start(bf16[4,4,2560]{2,1,0:T(4,128)(2,1)} %broadcast_in_dim.92), calls=%async_computation.1 | async-start | bytes 163840 | tf_op jit(solution)/shard_map/all_to_all | solution.py:479
  207.4 30.9 %collective-permute-start.4 = (f32[256,1280]{1,0:T(8,128)}, f32[256,1280]{1,0:T(8,128)S(1)}, u32[]{:S(2)}, u32[]{:S(2)}) collective-permute-start(f32[256,1280]{1,0:T(8,128)} %add.158), channel_id=1, source_target_pairs={{0,24},{8,0},{16,8},{24,16},{1,25},{9,1},{17,9},{25,17},{2,26},{10... | collective-permute-start | bytes 3932168 | tf_op jit(solution)/shard_map/ppermute | solution.py:561
  211.2 39.8 %collective-permute-start.1 = (f32[256,1280]{1,0:T(8,128)}, f32[256,1280]{1,0:T(8,128)}, u32[]{:S(2)}, u32[]{:S(2)}) collective-permute-start(f32[256,1280]{1,0:T(8,128)} %add.155), channel_id=1, source_target_pairs={{0,8},{8,16},{16,24},{24,0},{1,9},{9,17},{17,25},{25,1},{2,10},{10... | collective-permute-start | bytes 3932168 | tf_op jit(solution)/shard_map/ppermute | solution.py:560
  212.3 26.1 %copy-start.6 = (f32[256,1280]{1,0:T(8,128)S(1)}, f32[256,1280]{1,0:T(8,128)}, u32[]{:S(2)}) copy-start(f32[256,1280]{1,0:T(8,128)} %get-tuple-element.26) | copy-start | bytes 3932164
  239.5 47.0 %collective-permute-start.5 = (f32[256,1280]{1,0:T(8,128)}, f32[256,1280]{1,0:T(8,128)}, u32[]{:S(2)}, u32[]{:S(2)}) collective-permute-start(f32[256,1280]{1,0:T(8,128)} %add.159), channel_id=1, source_target_pairs={{0,24},{8,0},{16,8},{24,16},{1,25},{9,1},{17,9},{25,17},{2,26},{10... | collective-permute-start | bytes 3932168 | tf_op jit(solution)/shard_map/ppermute | solution.py:561
  247.4 40.9 %copy-start.2 = (f32[256,1280]{1,0:T(8,128)S(1)}, f32[256,1280]{1,0:T(8,128)}, u32[]{:S(2)}) copy-start(f32[256,1280]{1,0:T(8,128)} %get-tuple-element.27) | copy-start | bytes 3932164
  247.4 23.8 %all-to-all-start.2 = ((f32[4,4,2560]{2,1,0:T(4,128)}), f32[4,4,2560]{2,1,0:T(4,128)S(1)}, u32[]{:S(2)}, u32[]{:S(2)}) async-start(f32[4,4,2560]{2,1,0:T(4,128)} %fusion.4), calls=%async_computation.2 | async-start | bytes 327680 | tf_op jit(solution)/shard_map/all_to_all | solution.py:474
  253.6 36.2 %copy-start.1 = (f32[256,1280]{1,0:T(8,128)S(1)}, f32[256,1280]{1,0:T(8,128)}, u32[]{:S(2)}) copy-start(f32[256,1280]{1,0:T(8,128)} %get-tuple-element.23) | copy-start | bytes 3932164
  253.6 36.2 %collective-permute-start.2 = (f32[256,1280]{1,0:T(8,128)}, f32[256,1280]{1,0:T(8,128)}, u32[]{:S(2)}, u32[]{:S(2)}) collective-permute-start(f32[256,1280]{1,0:T(8,128)} %add.156), channel_id=1, source_target_pairs={{0,8},{8,16},{16,24},{24,0},{1,9},{9,17},{17,25},{25,1},{2,10},{10... | collective-permute-start | bytes 3932168 | tf_op jit(solution)/shard_map/ppermute | solution.py:560
  271.9 14.6 %all-to-all-start.3 = ((bf16[4,4,2560]{2,1,0:T(4,128)(2,1)}), bf16[4,4,2560]{2,1,0:T(4,128)(2,1)S(1)}, u32[]{:S(2)}, u32[]{:S(2)}) async-start(bf16[4,4,2560]{2,1,0:T(4,128)(2,1)} %broadcast_in_dim.94), calls=%async_computation.3 | async-start | bytes 163840 | tf_op jit(solution)/shard_map/all_to_all | solution.py:479
  286.5 16.1 %collective-permute-start.13 = (bf16[1,2,1024,128]{3,2,0,1:T(8,128)(2,1)S(1)}, bf16[1,2,1024,128]{3,2,0,1:T(8,128)(2,1)S(1)}, u32[]{:S(2)}, u32[]{:S(2)}) collective-permute-start(bf16[1,2,1024,128]{3,2,0,1:T(8,128)(2,1)S(1)} %get-tuple-element.52), channel_id=1, source_target_pairs={{0,28},{1,29},{2,30},{3,31},{4,24},{5,25},{6,26},{7,27},{8,4},{9,5... | collective-permute-start | bytes 1572872 | tf_op jit(solution)/shard_map/ppermute | solution.py:464
  292.9 29.4 %collective-permute-start.6 = (bf16[256,2560]{1,0:T(8,128)(2,1)S(1)}, bf16[256,2560]{1,0:T(8,128)(2,1)S(1)}, u32[]{:S(2)}, u32[]{:S(2)}) collective-permute-start(bf16[256,2560]{1,0:T(8,128)(2,1)S(1)} %add_convert_fusion.own), channel_id=1, source_target_pairs={{0,8},{8,16},{16,24},{24,0},{1,9},{9,17},{17,25},{25,1},{2,10},{10... | collective-permute-start | bytes 3932168 | tf_op jit(solution)/shard_map/ppermute | solution.py:447
  294.6 33.7 %collective-permute-start.7 = (bf16[256,2560]{1,0:T(8,128)(2,1)S(1)}, bf16[256,2560]{1,0:T(8,128)(2,1)}, u32[]{:S(2)}, u32[]{:S(2)}) collective-permute-start(bf16[256,2560]{1,0:T(8,128)(2,1)S(1)} %add_convert_fusion.own), channel_id=1, source_target_pairs={{0,24},{8,0},{16,8},{24,16},{1,25},{9,1},{17,9},{25,17},{2,26},{10... | collective-permute-start | bytes 3932168 | tf_op jit(solution)/shard_map/ppermute | solution.py:448
  322.3 14.5 %collective-permute-start.8 = (bf16[128,2560]{1,0:T(8,128)(2,1)S(1)}, bf16[128,2560]{1,0:T(8,128)(2,1)S(1)}, u32[]{:S(2)}, u32[]{:S(2)}) collective-permute-start(bf16[128,2560]{1,0:T(8,128)(2,1)S(1)} %slice.140), channel_id=1, source_target_pairs={{0,8},{8,16},{16,24},{24,0},{1,9},{9,17},{17,25},{25,1},{2,10},{10... | collective-permute-start | bytes 1966088 | tf_op jit(solution)/shard_map/ppermute | solution.py:449
  329.5 16.9 %collective-permute-start.9 = (bf16[128,2560]{1,0:T(8,128)(2,1)S(1)}, bf16[128,2560]{1,0:T(8,128)(2,1)S(1)}, u32[]{:S(2)}, u32[]{:S(2)}) collective-permute-start(bf16[128,2560]{1,0:T(8,128)(2,1)S(1)} %slice.141), channel_id=1, source_target_pairs={{0,24},{8,0},{16,8},{24,16},{1,25},{9,1},{17,9},{25,17},{2,26},{10... | collective-permute-start | bytes 1966088 | tf_op jit(solution)/shard_map/ppermute | solution.py:450
  (8 other events, 58.1 us)

commit v2 on v1

--- a/solution.py
+++ b/solution.py
@@ -31,15 +31,6 @@
     inv_freq = THETA ** (-jnp.arange(half_dim, dtype=jnp.float32) * 2.0 / head_dim)
     angles = positions.astype(jnp.float32)[:, None] * inv_freq[None, :]
     return jnp.cos(angles), jnp.sin(angles)
-
-
-def apply_rope(values_in, cos_tab, sin_tab):
-    half_dim = values_in.shape[-1] // 2
-    lower_half = values_in[..., :half_dim]
-    upper_half = values_in[..., half_dim:]
-    cos_b = cos_tab[:, None, :]
-    sin_b = sin_tab[:, None, :]
-    return jnp.concatenate([lower_half * cos_b - upper_half * sin_b, upper_half * cos_b + lower_half * sin_b], axis=-1)
 
 
 def front_kernel(len_ref, cos_ref, sin_ref, g1_ref, g2_ref, x_hbm, wqkv_hbm, wo_hbm, h_hbm, n_hbm, k_ref, v_ref, xs, ns, nv, wv, acc, qv, ctx, wo, wsem, xsem, osem, hsem, nsem, ssem, rsem, *, rb, tp_size, side_size):
@@ -344,225 +335,437 @@
     )(s_len, cos_full, sin_full, gain1, gain2, x, w_qkv, w_o)
 
 
-def mlp_kernel(idx_ref, n_hbm, wgu_hbm, wd_hbm, o0, o1, o2, o3, nv, gu_v, wd_v, acc, nsem, gsem, dsem, *, fb):
+def back_kernel(h_hbm, n_hbm, wgu_hbm, wd_hbm, k_hbm, v_hbm, tok_ref, len_ref, dcos_ref, dsin_ref, dg1_ref, dg2_ref, wqd_hbm, wod_hbm, wgud_hbm, wdd_hbm, kc_hbm, vc_hbm, out_hbm, kp_hbm, vp_hbm, dec_ref, ktok_ref, vtok_ref, nv, act, gu_v, wd_v, part, land, hb, hres, cbuf, dscr, dq, dprob, dctx, dpart, dland, dtok, dact, nsem, gsem, dsem, hsem, osem, qsem, dgsem, csem, ssem, rsem, *, fb, tp_size, side_size):
     ff, depth = wd_hbm.shape
-    chunk = o0.shape[0]
+    heads, rows, head_dim = k_hbm.shape
+    chunk = rows // tp_size
+    half = depth // 2
+    sub = half // 2
+    me = lax.axis_index('tp')
+    side = lax.axis_index('side')
+    tp_of = lambda d: lax.rem(me + d + tp_size, tp_size)
+    to_right = {'tp': tp_of(1)}
+    to_left = {'tp': tp_of(-1)}
+    mate = lax.rem(side + side_size // 2, side_size)
+    order = (-1, 1, 2, 0)
     pieces = [(f, min(fb, ff - f)) for f in range(0, ff, fb)]
+    sent = []
+
+    def start(copy):
+        copy.start()
+        sent.append(copy)
+
+    def remote(idx, src, dst, dev):
+        return pltpu.make_async_remote_copy(src_ref=src, dst_ref=dst, send_sem=ssem.at[idx], recv_sem=rsem.at[idx], device_id=dev, device_id_type=pl.DeviceIdType.MESH)
+
+    def rows_of(d):
+        return pl.ds(pl.multiple_of(tp_of(d) * chunk, chunk), chunk)
 
     def n_copy(c):
-        src = n_hbm.at[pl.ds(pl.multiple_of(idx_ref[c] * chunk, chunk), chunk), :]
-        return pltpu.make_async_copy(src, nv.at[pl.ds(c * chunk, chunk), :], nsem.at[c])
+        return pltpu.make_async_copy(n_hbm.at[rows_of(order[c]), :], nv.at[pl.ds(c * chunk, chunk), :], nsem.at[c])
 
     def gu_copy(p, which):
         f, size = pieces[p]
         return pltpu.make_async_copy(wgu_hbm.at[which, pl.ds(f, size), :], gu_v.at[which, pl.ds(f, size), :], gsem.at[2 * p + which])
 
-    def wd_copy(p):
-        f, size = pieces[p]
-        return pltpu.make_async_copy(wd_hbm.at[pl.ds(f, size), :], wd_v.at[pl.ds(f, size), :], dsem.at[p])
+    wd_copy = pltpu.make_async_copy(wd_hbm, wd_v, dsem.at[0])
+    h_copy = pltpu.make_async_copy(h_hbm.at[rows_of(0), :], hres, hsem.at[0])
 
     n_copy(0).start()
     n_copy(1).start()
-    for p in range(len(pieces)):
+    ahead = 3
+    for p in range(ahead):
         gu_copy(p, 0).start()
         gu_copy(p, 1).start()
-    for p in range(len(pieces)):
-        wd_copy(p).start()
+
+    barrier = pltpu.get_barrier_semaphore()
+    peers = [{'tp': tp_of(d)} for d in range(1, tp_size)] + [{'tp': t, 'side': mate} for t in range(tp_size)]
+    for dev in peers:
+        pl.semaphore_signal(barrier, inc=1, device_id=dev, device_id_type=pl.DeviceIdType.MESH)
+    pl.semaphore_wait(barrier, len(peers))
+
+    def kv_send(i, src, dst, idx):
+        head = me * heads + i
+        return remote(idx, src.at[i], dst.at[head // tp_size], {'tp': lax.rem(head, tp_size), 'side': mate})
+
+    def kv_land(i, src, dst, idx):
+        slot = lax.rem(me - i + heads, heads)
+        return remote(idx, src.at[i], dst.at[slot], {'tp': me, 'side': mate})
+
+    for i in range(heads):
+        start(kv_send(i, k_hbm, kp_hbm, i))
+        start(kv_send(i, v_hbm, vp_hbm, heads + i))
+    base = 2 * heads
+
+    nt = (((1,), (1,)), ((), ()))
+    span = 2 * chunk
+
+    def gate_up(c, f, size):
+        n_rows = nv[c * chunk:c * chunk + span, :]
+        gate = lax.dot_general(n_rows, gu_v[0, f:f + size, :], nt, preferred_element_type=jnp.float32)
+        up = lax.dot_general(n_rows, gu_v[1, f:f + size, :], nt, preferred_element_type=jnp.float32)
+        gate = gate.astype(jnp.bfloat16).astype(jnp.float32)
+        up = up.astype(jnp.bfloat16).astype(jnp.float32)
+        act[:, f:f + size] = (gate * jax.nn.sigmoid(gate) * up).astype(jnp.bfloat16)
+
+    def down(c, row, n_rows, lo):
+        for col in range(lo, lo + half, fb):
+            part[(c + row) * chunk:(c + row) * chunk + n_rows, col:col + fb] = jnp.dot(act[row * chunk:row * chunk + n_rows, :], wd_v[:, col:col + fb], preferred_element_type=jnp.float32)
+
     n_copy(0).wait()
     n_copy(1).wait()
-    nt = (((1,), (1,)), ((), ()))
     for p, (f, size) in enumerate(pieces):
         gu_copy(p, 0).wait()
         gu_copy(p, 1).wait()
-        gate = lax.dot_general(nv[...], gu_v[0, f:f + size, :], nt, preferred_element_type=jnp.float32)
-        up = lax.dot_general(nv[...], gu_v[1, f:f + size, :], nt, preferred_element_type=jnp.float32)
-        gate = gate.astype(jnp.bfloat16).astype(jnp.float32)
-        up = up.astype(jnp.bfloat16).astype(jnp.float32)
-        acc[:, f:f + size] = (gate * jax.nn.sigmoid(gate) * up).astype(jnp.bfloat16)
-    for p in range(len(pieces)):
-        wd_copy(p).wait()
-    half = depth // 2
-    for lo, top, low in ((0, o0, o2), (half, o1, o3)):
-        for c in range(0, half, fb):
-            part = jnp.dot(acc[...], wd_v[:, lo + c:lo + c + fb], preferred_element_type=jnp.float32)
-            top[:, c:c + fb] = part[:chunk]
-            low[:, c:c + fb] = part[chunk:]
-
-
-def mlp_call(idx, normed, w_gu, w_down, chunk):
-    ff, depth = w_down.shape
+        if p + ahead < len(pieces):
+            gu_copy(p + ahead, 0).start()
+            gu_copy(p + ahead, 1).start()
+        if p + ahead == len(pieces):
+            wd_copy.start()
+            n_copy(2).start()
+            n_copy(3).start()
+            h_copy.start()
+        gate_up(0, f, size)
+    wd_copy.wait()
+
+    cols = lambda way, q: pl.ds(way * half + q * sub, sub)
+    devs = (to_right, to_left)
+
+    def rs(step, way, q):
+        idx = base + 4 * step + 2 * way + q
+        dst = land.at[step, :, cols(way, q)]
+        if step == 0:
+            src = part.at[pl.ds(way * chunk, chunk), cols(way, q)]
+        else:
+            src = land.at[step - 1, :, cols(way, q)]
+        return remote(idx, src, dst, devs[way])
+
+    down(0, 0, chunk, 0)
+    start(rs(0, 0, 0))
+    start(rs(0, 0, 1))
+    down(0, 1, chunk, half)
+    start(rs(0, 1, 0))
+    start(rs(0, 1, 1))
+    down(0, 0, chunk, half)
+    down(0, 1, chunk, 0)
+    n_copy(2).wait()
+    n_copy(3).wait()
+    for f, size in pieces:
+        gate_up(2, f, size)
+    d_rows = tok_ref.shape[0]
+    d_heads = heads
+    shard = heads * head_dim
+    n_kind = wqd_hbm.shape[0]
+    cache_len = kc_hbm.shape[2]
+    k_half = depth // 2
+    lo_rows = 3 * head_dim
+
+    def wq_copy(kind, head, hv):
+        idx = kind * d_heads + head
+        return pltpu.make_async_copy(wqd_hbm.at[kind, head, pl.ds(hv * k_half, k_half), :], gu_v.at[hv, pl.ds(0, k_half), pl.ds(idx * head_dim, head_dim)], qsem.at[2 * idx + hv])
+
+    wo_lo = pltpu.make_async_copy(wod_hbm.at[pl.ds(0, lo_rows), :], gu_v.at[0, pl.ds(k_half, lo_rows), :], dsem.at[1])
+    wo_hi = pltpu.make_async_copy(wod_hbm.at[pl.ds(lo_rows, shard - lo_rows), :], gu_v.at[1, pl.ds(k_half, shard - lo_rows), :], dsem.at[2])
+    wdd_copy = pltpu.make_async_copy(wdd_hbm, wd_v, dsem.at[3])
+
+    def gud_copy(p, which):
+        f, size = pieces[p]
+        return pltpu.make_async_copy(wgud_hbm.at[which, pl.ds(f, size), :], gu_v.at[which, pl.ds(f, size), :], dgsem.at[2 * p + which])
+
+    def c_copy(src, b, slot):
+        return pltpu.make_async_copy(src.at[b], cbuf.at[slot], csem.at[slot])
+
+    for kind in range(n_kind):
+        for head in range(d_heads):
+            for hv in range(2):
+                wq_copy(kind, head, hv).start()
+    wo_lo.start()
+    wo_hi.start()
+    c_copy(kc_hbm, 0, 0).start()
+    down(2, 0, span, 0)
+    down(2, 0, span, half)
+    wdd_copy.start()
+
+    nb = 64
+    slots = ((2, 2), (1, 0), (3, 3))
+
+    def event(step, q):
+        for way in range(2):
+            rs(step, way, q).wait_recv()
+
+            def add_step(i, carry, way=way):
+                r = pl.ds(pl.multiple_of(i * nb, nb), nb)
+                pr = pl.ds(pl.multiple_of(slots[step][way] * chunk + i * nb, nb), nb)
+                land[step, r, cols(way, q)] += part[pr, cols(way, q)]
+                return carry
+
+            lax.fori_loop(0, chunk // nb, add_step, 0)
+            start(rs(step + 1, way, q))
+
+    def decode_qkv():
+        normed = rms_norm(tok_ref[...], dg1_ref[...])
+        for kind in range(n_kind):
+            for head in range(d_heads):
+                for hv in range(2):
+                    wq_copy(kind, head, hv).wait()
+        cos_b = dcos_ref[...]
+        sin_b = dsin_ref[...]
+        for kind in range(n_kind):
+            c0 = kind * shard
+            val = jnp.dot(normed[:, :k_half], gu_v[0, 0:k_half, c0:c0 + shard], preferred_element_type=jnp.float32)
+            val += jnp.dot(normed[:, k_half:], gu_v[1, 0:k_half, c0:c0 + shard], preferred_element_type=jnp.float32)
+            for head in range(d_heads):
+                one = val[:, head * head_dim:(head + 1) * head_dim]
+                if kind < 2:
+                    one = one * cos_b + pltpu.roll(one, head_dim // 2, 1) * sin_b
+                (dq, ktok_ref, vtok_ref)[kind][head] = one.astype(jnp.bfloat16)
+
+    row_id = lax.broadcasted_iota(jnp.int32, (d_rows, 1), 0)
+
+    def over_rows(src, body):
+        def step(b, carry):
+            slot = lax.rem(b, 2)
+            c_copy(src, b, slot).wait()
+
+            @pl.when(b + 1 < d_rows)
+            def _():
+                c_copy(src, b + 1, 1 - slot).start()
+
+            body(b, slot)
+            return carry
+
+        lax.fori_loop(0, d_rows, step, 0)
+
+    def decode_scores():
+        def body(b, slot):
+            for head in range(d_heads):
+                sc = lax.dot_general(dq[head], cbuf[slot, head], nt, preferred_element_type=jnp.float32)
+                dscr[head] = jnp.where(row_id == b, sc, dscr[head])
+
+        over_rows(kc_hbm, body)
+        c_copy(vc_hbm, 0, 0).start()
+        scale = head_dim ** -0.5
+        pos = lax.broadcasted_iota(jnp.int32, (d_rows, cache_len), 1)
+        seen = pos < len_ref[...]
+        for head in range(d_heads):
+            sc = jnp.where(seen, dscr[head] * scale, MASKED)
+            own_sc = jnp.sum(dq[head].astype(jnp.float32) * ktok_ref[head].astype(jnp.float32), axis=-1, keepdims=True) * scale
+            top = jnp.maximum(jnp.max(sc, axis=-1, keepdims=True), own_sc)
+            ex = jnp.exp(sc - top)
+            own_ex = jnp.exp(own_sc - top)
+            den = jnp.sum(ex, axis=-1, keepdims=True) + own_ex
+            dprob[head] = (ex / den).astype(jnp.bfloat16)
+            own_p = (own_ex / den).astype(jnp.bfloat16).astype(jnp.float32)
+            dctx[:, head * head_dim:(head + 1) * head_dim] = own_p * vtok_ref[head].astype(jnp.float32)
+
+    def decode_context():
+        def body(b, slot):
+            for head in range(d_heads):
+                got = jnp.dot(dprob[head], cbuf[slot, head], preferred_element_type=jnp.float32)
+                hc = slice(head * head_dim, (head + 1) * head_dim)
+                dctx[:, hc] += jnp.where(row_id == b, got, 0.0)
+
+        over_rows(vc_hbm, body)
+        wo_lo.wait()
+        wo_hi.wait()
+        ctx_b = dctx[...].astype(jnp.bfloat16)
+        val = jnp.dot(ctx_b[:, :lo_rows], gu_v[0, k_half:k_half + lo_rows, :], preferred_element_type=jnp.float32)
+        dpart[0] = val + jnp.dot(ctx_b[:, lo_rows:], gu_v[1, k_half:k_half + shard - lo_rows, :], preferred_element_type=jnp.float32)
+        for p in range(len(pieces)):
+            gud_copy(p, 0).start()
+            gud_copy(p, 1).start()
+
+    base_d = base + 24
+    d_cols = lambda d: pl.ds(pl.multiple_of(tp_of(d) * shard, 128), shard)
+
+    def d_scatter(n, d):
+        return remote(base_d + 6 * n + d - 1, dpart.at[n, :, d_cols(d)], dland.at[n, d - 1], {'tp': tp_of(d)})
+
+    def d_gather(n, d):
+        return remote(base_d + 6 * n + 2 + d, dtok.at[n, :, d_cols(0)], dtok.at[n, :, d_cols(0)], {'tp': tp_of(d)})
+
+    def d_gather_land(n, d):
+        return remote(base_d + 6 * n + 2 + d, dtok.at[n, :, d_cols(-d)], dtok.at[n, :, d_cols(-d)], {'tp': tp_of(d)})
+
+    def decode_scatter(n):
+        for d in range(1, tp_size):
+            start(d_scatter(n, d))
+
+    def decode_sum(n, before):
+        for d in range(1, tp_size):
+            d_scatter(n, d).wait_recv()
+        total = dpart[n, :, d_cols(0)]
+        for d in range(1, tp_size):
+            total = total + dland[n, d - 1]
+        dtok[n, :, d_cols(0)] = add_residual(before[:, d_cols(0)], total.astype(jnp.bfloat16))
+        for d in range(1, tp_size):
+            start(d_gather(n, d))
+
+    def decode_gathered(n):
+        for d in range(1, tp_size):
+            d_gather_land(n, d).wait_recv()
+
+    def decode_gate_up():
+        normed = rms_norm(dtok[0], dg2_ref[...])
+        for p, (f, size) in enumerate(pieces):
+            gud_copy(p, 0).wait()
+            gud_copy(p, 1).wait()
+            gate = lax.dot_general(normed, gu_v[0, f:f + size, :], nt, preferred_element_type=jnp.float32)
+            up = lax.dot_general(normed, gu_v[1, f:f + size, :], nt, preferred_element_type=jnp.float32)
+            gate = gate.astype(jnp.bfloat16).astype(jnp.float32)
+            up = up.astype(jnp.bfloat16).astype(jnp.float32)
+            dact[:, f:f + size] = (gate * jax.nn.sigmoid(gate) * up).astype(jnp.bfloat16)
+
+    def decode_down():
+        wdd_copy.wait()
+        dpart[1] = jnp.dot(dact[...], wd_v[...], preferred_element_type=jnp.float32)
+
+    event(0, 0)
+    decode_qkv()
+    event(0, 1)
+    decode_scores()
+    decode_context()
+    decode_scatter(0)
+    event(1, 0)
+    decode_sum(0, tok_ref)
+    event(1, 1)
+    decode_gathered(0)
+    decode_gate_up()
+    decode_down()
+    decode_scatter(1)
+
+    base_ag = base + 12
+    h_copy.wait()
+
+    def ag(way, q, dev_i):
+        idx = base_ag + 4 * way + 2 * q + dev_i
+        return remote(idx, hb.at[:, cols(way, q)], out_hbm.at[rows_of(0), cols(way, q)], devs[dev_i])
+
+    def ag_land(way, q, dev_i):
+        idx = base_ag + 4 * way + 2 * q + dev_i
+        return remote(idx, hb.at[:, cols(way, q)], out_hbm.at[rows_of(-1 if dev_i == 0 else 1), cols(way, q)], devs[dev_i])
+
+    def fwd(way, q):
+        ref = out_hbm.at[rows_of(-1 if way == 0 else 1), cols(way, q)]
+        return remote(base_ag + 8 + 2 * way + q, ref, ref, devs[way])
+
+    def fwd_land(way, q):
+        ref = out_hbm.at[rows_of(2), cols(way, q)]
+        return remote(base_ag + 8 + 2 * way + q, ref, ref, devs[way])
+
+    for q in range(2):
+        for way in range(2):
+            rs(2, way, q).wait_recv()
+
+            def end_step(i, carry, way=way, q=q):
+                r = pl.ds(pl.multiple_of(i * nb, nb), nb)
+                pr = pl.ds(pl.multiple_of(3 * chunk + i * nb, nb), nb)
+                total = land[2, r, cols(way, q)] + part[pr, cols(way, q)]
+                hb[r, cols(way, q)] = add_residual(hres[r, cols(way, q)], total.astype(jnp.bfloat16))
+                return carry
+
+            lax.fori_loop(0, chunk // nb, end_step, 0)
+            start(ag(way, q, way))
+            start(ag(way, q, 1 - way))
+        if q == 0:
+            decode_sum(1, dtok.at[0])
+    own = pltpu.make_async_copy(hb, out_hbm.at[rows_of(0), :], osem.at[0])
+    own.start()
+    for q in range(2):
+        for way in range(2):
+            ag_land(way, q, way).wait_recv()
+            start(fwd(way, q))
+    for q in range(2):
+        for way in range(2):
+            ag_land(way, q, 1 - way).wait_recv()
+    for i in range(heads):
+        kv_land(i, k_hbm, kp_hbm, i).wait_recv()
+        kv_land(i, v_hbm, vp_hbm, heads + i).wait_recv()
+    for q in range(2):
+        for way in range(2):
+            fwd_land(way, q).wait_recv()
+    own.wait()
+    decode_gathered(1)
+    dec_ref[...] = dtok[1]
+    for copy in sent:
+        copy.wait_send()
+
+
+def back_call(h, normed, w_gu, w_down, k, v, dec, tp_size, side_size):
+    rows, depth = h.shape
+    ff = w_down.shape[0]
+    heads = k.shape[0]
+    chunk = rows // tp_size
     fb = 256
     n_piece = -(-ff // fb)
-    out = jax.ShapeDtypeStruct((chunk, depth // 2), jnp.float32)
+    n_msg = 2 * heads + 12 + 12 + 12
+    d_rows = dec[0].shape[0]
+    head_dim = k.shape[2]
+    cache_len = dec[10].shape[2]
+    dma = pltpu.SemaphoreType.DMA
+    bf16 = jnp.bfloat16
+    kv = jax.ShapeDtypeStruct(k.shape, bf16)
     return pl.pallas_call(
-        functools.partial(mlp_kernel, fb=fb),
-        out_shape=(out,) * 4,
-        in_specs=[SM, ANY, ANY, ANY],
-        out_specs=(VM,) * 4,
+        functools.partial(back_kernel, fb=fb, tp_size=tp_size, side_size=side_size),
+        out_shape=(jax.ShapeDtypeStruct((rows, depth), bf16), kv, kv, jax.ShapeDtypeStruct((d_rows, depth), bf16)) + (jax.ShapeDtypeStruct((heads, d_rows, head_dim), bf16),) * 2,
+        in_specs=[ANY] * 6 + [VM] * 6 + [ANY] * 6,
+        out_specs=(ANY,) * 3 + (VM,) * 3,
         scratch_shapes=[
-            pltpu.VMEM((2 * chunk, depth), jnp.bfloat16),
-            pltpu.VMEM((2, ff, depth), jnp.bfloat16),
-            pltpu.VMEM((ff, depth), jnp.bfloat16),
-            pltpu.VMEM((2 * chunk, ff), jnp.bfloat16),
-            pltpu.SemaphoreType.DMA((2,)),
-            pltpu.SemaphoreType.DMA((2 * n_piece,)),
-            pltpu.SemaphoreType.DMA((n_piece,)),
+            pltpu.VMEM((rows, depth), bf16),
+            pltpu.VMEM((2 * chunk, ff), bf16),
+            pltpu.VMEM((2, ff, depth), bf16),
+            pltpu.VMEM((ff, depth), bf16),
+            pltpu.VMEM((rows, depth), jnp.float32),
+            pltpu.VMEM((3, chunk, depth), jnp.float32),
+            pltpu.VMEM((chunk, depth), bf16),
+            pltpu.VMEM((chunk, depth), bf16),
+            pltpu.VMEM((2, heads, cache_len, head_dim), bf16),
+            pltpu.VMEM((heads, d_rows, cache_len), jnp.float32),
+            pltpu.VMEM((heads, d_rows, head_dim), bf16),
+            pltpu.VMEM((heads, d_rows, cache_len), bf16),
+            pltpu.VMEM((d_rows, heads * head_dim), jnp.float32),
+            pltpu.VMEM((2, d_rows, depth), jnp.float32),
+            pltpu.VMEM((2, tp_size - 1, d_rows, heads * head_dim), jnp.float32),
+            pltpu.VMEM((2, d_rows, depth), bf16),
+            pltpu.VMEM((d_rows, ff), bf16),
+            dma((tp_size,)), dma((2 * n_piece,)), dma((4,)), dma((1,)), dma((1,)), dma((6 * heads,)), dma((2 * n_piece,)), dma((2,)), dma((n_msg,)), dma((n_msg,)),
         ],
-        compiler_params=pltpu.CompilerParams(vmem_limit_bytes=VMEM_LIMIT),
-        cost_estimate=pl.CostEstimate(flops=12 * chunk * ff * depth, bytes_accessed=6 * ff * depth + 12 * chunk * depth, transcendentals=0),
-        name="mlp",
-    )(idx, normed, w_gu, w_down)
-
-
-def assemble_kernel(own, left, right, top, low, out, sems, *, tp_size):
-    rows = own.shape[0]
-    half = rows // 2
-    me = lax.axis_index('tp')
-    spot = lambda d, off: pl.multiple_of(lax.rem(me + d + tp_size, tp_size) * rows + off, half)
-    places = ((own, 0, 0, rows), (left, -1, 0, rows), (right, 1, 0, rows), (top, 2, 0, half), (low, 2, half, half))
-    copies = [pltpu.make_async_copy(ref, out.at[pl.ds(spot(d, off), size), :], sems.at[n]) for n, (ref, d, off, size) in enumerate(places)]
-    for copy in copies:
-        copy.start()
-    for copy in copies:
-        copy.wait()
-
-
-def assemble_call(own, left, right, top, low, tp_size):
-    rows, width = own.shape
-    return pl.pallas_call(
-        functools.partial(assemble_kernel, tp_size=tp_size),
-        out_shape=jax.ShapeDtypeStruct((tp_size * rows, width), own.dtype),
-        in_specs=[VM] * 5,
-        out_specs=ANY,
-        scratch_shapes=[pltpu.SemaphoreType.DMA((5,))],
-        compiler_params=pltpu.CompilerParams(vmem_limit_bytes=32 * 1024 * 1024),
-        cost_estimate=pl.CostEstimate(flops=rows * width, bytes_accessed=16 * rows * width, transcendentals=0),
-        name="assemble",
-    )(own, left, right, top, low)
-
-
-def ring_gather(block, right, left, me, tp_size):
-    rows = block.shape[0]
-    half = rows // 2
-    from_left = lax.ppermute(block, 'tp', right)
-    from_right = lax.ppermute(block, 'tp', left)
-    far_top = lax.ppermute(from_left[:half], 'tp', right)
-    far_low = lax.ppermute(from_right[half:], 'tp', left)
-    return assemble_call(block, from_left, from_right, far_top, far_low, tp_size)
-
-
-def move_kv(k, v, me, tp_size, side_size):
-    heads = k.shape[0]
-    kv = jnp.stack([k, v], axis=1)
-    pieces = []
-    for off in range(tp_size):
-        group = list(range(off, heads, tp_size))
-        perm = []
-        for t in range(tp_size):
-            for s in range(side_size):
-                perm.append((t * side_size + s, (t + off) % tp_size * side_size + (s + side_size // 2) % side_size))
-        got = lax.ppermute(jnp.stack([kv[i] for i in group]), ('tp', 'side'), perm)
-        pieces.extend((group[n], got[n]) for n in range(len(group)))
-    stacked = jnp.stack([piece for _, piece in sorted(pieces, key=lambda item: item[0])])
-    head_ids = jnp.arange(heads) * tp_size + me
-    picked = jnp.take(stacked, head_ids % heads, axis=0)
-    return picked[:, 0], picked[:, 1]
-
-
-def small_psum(part, tp_size):
-    rows, width = part.shape
-    blocks = lax.all_to_all(part.reshape(tp_size, rows // tp_size, width), 'tp', 0, 0)
-    total = blocks[0]
-    for i in range(1, tp_size):
-        total = total + blocks[i]
-    mine = jnp.broadcast_to(total.astype(jnp.bfloat16)[None], (tp_size, rows // tp_size, width))
-    return lax.all_to_all(mine, 'tp', 0, 0).reshape(rows, width)
-
-
-def swiglu(hidden, gain_vec, w_gu, w_down):
-    normed = rms_norm(hidden, gain_vec)
-    gate_up = jnp.einsum('...d,kfd->...kf', normed, w_gu, preferred_element_type=jnp.float32)
-    gate_val = gate_up[..., 0, :].astype(jnp.bfloat16).astype(jnp.float32)
-    up_val = gate_up[..., 1, :].astype(jnp.bfloat16).astype(jnp.float32)
-    activated = (jax.nn.silu(gate_val) * up_val).astype(jnp.bfloat16)
-    return jnp.einsum('...f,fd->...d', activated, w_down, preferred_element_type=jnp.float32)
-
-
-def decode_attention(queries, k_tok, v_tok, k_layer, v_layer, visible):
-    attn_scale = queries.shape[-1] ** -0.5
-    cache_scores = jnp.einsum('bhe,bthe->bht', queries, k_layer, preferred_element_type=jnp.float32) * attn_scale
-    cache_scores = jnp.where(visible, cache_scores, MASKED)
-    self_score = jnp.einsum('bhe,bhe->bh', queries, k_tok, preferred_element_type=jnp.float32) * attn_scale
-    row_max = jnp.maximum(jnp.max(cache_scores, axis=-1), self_score)
-    cache_exp = jnp.exp(cache_scores - row_max[..., None])
-    self_exp = jnp.exp(self_score - row_max)
-    denominator = jnp.sum(cache_exp, axis=-1) + self_exp
-    cache_prob = (cache_exp / denominator[..., None]).astype(jnp.bfloat16)
-    self_prob = (self_exp / denominator).astype(jnp.bfloat16).astype(jnp.float32)
-    context = jnp.einsum('bht,bthe->bhe', cache_prob, v_layer, preferred_element_type=jnp.float32) + self_prob[..., None] * v_tok.astype(jnp.float32)
-    return context.astype(jnp.bfloat16)
-
-
-def run_decode(tokens, k_cache, v_cache, c_len, w_qkv, w_out, w_gu, w_down, gains, tp_size):
-    layers, row_count, cache_len, heads_loc, _, head_dim = k_cache.shape
-    model_width = tokens.shape[1]
-    k_local = k_cache.reshape(layers, row_count, cache_len, heads_loc, head_dim)
-    v_local = v_cache.reshape(layers, row_count, cache_len, heads_loc, head_dim)
-    wqkv_local = w_qkv.reshape(layers, model_width, 3, heads_loc, head_dim)
-    wout_local = w_out.reshape(layers, heads_loc, head_dim, model_width)
-    cos_tab, sin_tab = rope_tables(c_len, head_dim)
-    cache_pos = jnp.arange(cache_len)
-    visible = (cache_pos[None, :] < c_len[:, None])[:, None, :]
-    write_at = (cache_pos[None, :] == c_len[:, None])[:, :, None, None]
-    k_next = []
-    v_next = []
-    for layer_idx in range(layers):
-        normed = rms_norm(tokens, gains[layer_idx, 0])
-        qkv_out = jnp.einsum('bd,dkhe->bkhe', normed, wqkv_local[layer_idx], preferred_element_type=jnp.float32)
-        queries = apply_rope(qkv_out[:, 0], cos_tab, sin_tab).astype(jnp.bfloat16)
-        k_tok = apply_rope(qkv_out[:, 1], cos_tab, sin_tab).astype(jnp.bfloat16)
-        v_tok = qkv_out[:, 2].astype(jnp.bfloat16)
-        context = decode_attention(queries, k_tok, v_tok, k_local[layer_idx], v_local[layer_idx], visible)
-        part_sum = jnp.einsum('bhe,hed->bd', context, wout_local[layer_idx], preferred_element_type=jnp.float32)
-        tokens = add_residual(tokens, small_psum(part_sum, tp_size))
-        mlp_part = swiglu(tokens, gains[layer_idx, 1], w_gu[layer_idx], w_down[layer_idx])
-        tokens = add_residual(tokens, small_psum(mlp_part, tp_size))
-        k_next.append(jnp.where(write_at, k_tok[:, None], k_local[layer_idx]))
-        v_next.append(jnp.where(write_at, v_tok[:, None], v_local[layer_idx]))
-    return tokens, jnp.stack(k_next).reshape(k_cache.shape), jnp.stack(v_next).reshape(v_cache.shape)
-
-
-def run_prefill(prompt, s_len, w_qkv, w_out, w_gu, w_down, gains, tp_size, side_size):
+        compiler_params=pltpu.CompilerParams(vmem_limit_bytes=67043328, collective_id=1, has_side_effects=True),
+        cost_estimate=pl.CostEstimate(flops=6 * rows * ff * depth, bytes_accessed=6 * ff * depth + 8 * rows * depth, transcendentals=0),
+        name="back",
+    )(h, normed, w_gu, w_down, k, v, *dec)
+
+
+def write_cache(cache, new, at):
+    row_count, cache_len = cache.shape[:2]
+    here = (jnp.arange(cache_len)[None, :] == at[:, None])[:, :, None, None, None]
+    return jnp.where(here, new.transpose(1, 0, 2)[:, None, :, None, :], cache)
+
+
+def run_layers(prompt, s_len, pre, tokens, k_cache, v_cache, c_len, dec, tp_size, side_size):
+    w_qkv, w_out, w_gu, w_down, gains = pre
+    dw_qkv, dw_out, dw_gu, dw_down, dgains = dec
     rows, width = prompt.shape
     layers, _, _, heads_loc, head_dim = w_qkv.shape
-    me = lax.axis_index('tp')
-    right = [(i, (i + 1) % tp_size) for i in range(tp_size)]
-    left = [(i, (i - 1) % tp_size) for i in range(tp_size)]
-    cos_tab, sin_tab = rope_tables(jnp.arange(rows), head_dim)
-    cos_full = jnp.concatenate([cos_tab, cos_tab], axis=-1)
-    sin_full = jnp.concatenate([-sin_tab, sin_tab], axis=-1)
-    chunk = rows // tp_size
-    half = width // 2
-    ids = (me + jnp.array([-1, 1, 2, 0], jnp.int32)) % tp_size
+    shard = heads_loc * head_dim
+    d_rows, cache_len = k_cache.shape[1:3]
+
+    def full_tables(positions):
+        cos_tab, sin_tab = rope_tables(positions, head_dim)
+        return jnp.concatenate([cos_tab, cos_tab], axis=-1), jnp.concatenate([-sin_tab, sin_tab], axis=-1)
+
+    cos_full, sin_full = full_tables(jnp.arange(rows))
+    d_cos, d_sin = full_tables(c_len)
     hidden = prompt
-    kv_layers = []
+    outs = []
     for layer in range(layers):
-        shard = heads_loc * head_dim
-        w_o = w_out[layer].reshape(shard, width)
         w_t = w_qkv[layer].transpose(1, 2, 0, 3)
-        hidden, normed, k, v = front_call(hidden, s_len, gains[layer, 0][None], gains[layer, 1][None], cos_full, sin_full, w_t, w_o, tp_size, side_size)
-        kv_layers.append(move_kv(k, v, me, tp_size, side_size))
-        a = mlp_call(ids[:2], normed, w_gu[layer], w_down[layer], chunk)
-        b = mlp_call(ids[2:], normed, w_gu[layer], w_down[layer], chunk)
-        go_r = a[0]
-        go_l = a[3]
-        for own_r, own_l in ((b[0], b[1]), (a[2], a[1]), (b[2], b[3])):
-            go_r = lax.ppermute(go_r, 'tp', right) + own_r
-            go_l = lax.ppermute(go_l, 'tp', left) + own_l
-        mine = lax.dynamic_slice_in_dim(hidden, me * chunk, chunk, 0)
-        down = jnp.concatenate([go_r, go_l], axis=1).astype(jnp.bfloat16)
-        hidden = ring_gather(add_residual(mine, down), right, left, me, tp_size)
-    return hidden, kv_layers
+        hidden, normed, k, v = front_call(hidden, s_len, gains[layer, 0][None], gains[layer, 1][None], cos_full, sin_full, w_t, w_out[layer].reshape(shard, width), tp_size, side_size)
+        by_head = lambda cache: cache[layer].reshape(d_rows, cache_len, heads_loc, head_dim).transpose(0, 2, 1, 3)
+        dec_args = (tokens, c_len[:, None], d_cos, d_sin, dgains[layer, 0][None], dgains[layer, 1][None], dw_qkv[layer].reshape(width, 3, heads_loc, head_dim).transpose(1, 2, 0, 3), dw_out[layer].reshape(shard, width), dw_gu[layer], dw_down[layer], by_head(k_cache), by_head(v_cache))
+        hidden, k_inst, v_inst, tokens, k_tok, v_tok = back_call(hidden, normed, w_gu[layer], w_down[layer], k, v, dec_args, tp_size, side_size)
+        outs.append((k_inst.transpose(1, 0, 2)[:, :, None, :], v_inst.transpose(1, 0, 2)[:, :, None, :], write_cache(k_cache[layer], k_tok, c_len), write_cache(v_cache[layer], v_tok, c_len)))
+    return (hidden, tokens) + tuple(jnp.stack(parts) for parts in zip(*outs))
 
 
 def solution(mesh):
@@ -577,10 +780,8 @@
     out_specs = (rows_spec, rows_spec, prompt_spec, prompt_spec, cache_spec, cache_spec)
 
     def device_fn(prompt_x, s_len, w_qkv_pre, w_out_pre, w_gu_pre, w_down_pre, gain_pre, dec_tokens, k_cache, v_cache, c_len, w_qkv_dec, w_out_dec, w_gu_dec, w_down_dec, gain_dec):
-        hidden, kv_layers = run_prefill(prompt_x, s_len, w_qkv_pre, w_out_pre, w_gu_pre, w_down_pre, gain_pre, tp_size, side_size)
-        k_prompt = jnp.stack([k for k, _ in kv_layers]).transpose(0, 2, 1, 3)[:, :, :, None, :]
-        v_prompt = jnp.stack([v for _, v in kv_layers]).transpose(0, 2, 1, 3)[:, :, :, None, :]
-        dec_out, k_cache_new, v_cache_new = run_decode(dec_tokens, k_cache, v_cache, c_len, w_qkv_dec, w_out_dec, w_gu_dec, w_down_dec, gain_dec, tp_size)
-        return hidden, dec_out, k_prompt, v_prompt, k_cache_new, v_cache_new
+        pre = (w_qkv_pre, w_out_pre, w_gu_pre, w_down_pre, gain_pre)
+        dec = (w_qkv_dec, w_out_dec, w_gu_dec, w_down_dec, gain_dec)
+        return run_layers(prompt_x, s_len, pre, dec_tokens, k_cache, v_cache, c_len, dec, tp_size, side_size)
 
     return jax.shard_map(device_fn, mesh=mesh, in_specs=in_specs, out_specs=out_specs, check_vma=False)

time: 355 us -> 308 us (0.87)
  the two profiles are of different devices: /device:TPU:96 before, /device:TPU:97 now
where the time goes in v2:
time: 308 us; the launch traced here: 304 us
  Pallas kernels  276 us (90%)
  other arithmetic  15.4 us (5%)
  local copies, waits for them, and re-layouts  11.1 us (4%)
    pallas_call x1, Pallas kernels, back_call(): pl.pallas_call(functools.partial(back_kernel, fb=fb, tp_size=tp_size, sid...  182 us
    pallas_call x1, Pallas kernels, front_call(): pl.pallas_call(functools.partial(front_kernel, rb=rb, tp_size=tp_size, si...  93.8 us
    select_n x1, other arithmetic, write_cache(): return jnp.where(here, new.transpose(1, 0, 2)[:, None, :, None, :], cache)  9.31 us

profile of v2, /device:TPU:97, one launch (start us, length us, event | category | flops | bytes accessed | tf_op | source)
XLA Modules:
  0.0 304.2 jit_solution(12546978235257175282)
XLA Ops:
  1.3 0.0 copy-start.4
  1.3 1.9 fusion
  3.2 0.0 copy-done.4
  3.2 1.3 pad_maximum_fusion
  4.5 1.4 slice_bitcast_fusion.2
  6.0 93.8 %front.1 = (bf16[1024,2560]{1,0:T(8,128)(2,1)}, bf16[1024,2560]{1,0:T(8,128)(2,1)}, bf16[5,1024,128]{2,1,0:T(8,128)(2,1)}, bf16[5,1024,128]{2,1,0:T(8,128)(2,1)}) custom-call(s32[1]{0:T(128)S(6)} %copy.31.len_ref, f32[1024,128]{1,0:T(8,128)} %get-tuple-element.44.cos_ref, f32[1024,128]{1,0:T(8,128)} %get-tuple-element.45.sin_ref, ...), custom_call_target="tpu_custom_call" | custom-call | flops 23488102400 | bytes 30801920 | tf_op jit(solution)/shard_map/front/pallas_call | solution.py:316
  99.7 1.3 copy.22.len_ref
  101.1 0.7 convert_element_type.17
  101.7 0.8 fusion.1
  102.5 0.7 pad_maximum_fusion.2
  103.2 1.4 slice_bitcast_fusion
  104.6 182.4 %back.1 = (bf16[1024,2560]{1,0:T(8,128)(2,1)}, bf16[5,1024,128]{2,1,0:T(8,128)(2,1)}, bf16[5,1024,128]{2,1,0:T(8,128)(2,1)}, bf16[16,2560]{1,0:T(8,128)(2,1)}, b...) custom-call(bf16[1024,2560]{1,0:T(8,128)(2,1)} %get-tuple-element.16.h_hbm, ...), custom_call_target="tpu_custom_call" | custom-call | flops 27179089920 | bytes 47513600 | tf_op jit(solution)/shard_map/back/pallas_call | solution.py:708
  287.0 0.7 iota_compare_fusion
  287.7 0.7 copy.24
  288.5 0.7 copy.23
  289.2 0.0 copy-start
  289.2 9.3 %broadcast_select_fusion = (bf16[1,16,256,5,1,128]{5,2,4,3,1,0:T(8,128)(2,1)}, bf16[1,16,256,5,1,128]{5,2,4,3,1,0:T(8,128)(2,1)}) fusion(bf16[1,16,256,5,1,128]{5,2,4,3,1,0:T(8,128)(2,1)} %param.25, pred[16,256]{1,0:T(8,128)(4,1)S(1)} %iota_compare_fusion, bf16[16,5,128]{2,1,0:T(8,128)(2,1)S(1)} %copy.24, bf16[1,16,256,5,1,128]{5,2,4,3,1,0:T(8,128)(2,1)} %param.24, ...), kind=kLoop, calls=%fused_computation | loop fusion | flops 5242880 | bytes 21016576 | tf_op jit(solution)/shard_map/jit(_where)/select_n | solution.py:742
  298.5 0.0 copy-start.2
  298.6 0.0 copy-start.1
  298.6 2.7 copy.32
  301.2 0.6 copy.33
  301.9 0.0 copy-done.2
  301.9 1.1 copy.34
  302.9 1.1 copy.35
  (6 shorter events, 0.0 us)
Async XLA Ops:
  1.3 1.9 copy-start.4
  289.2 9.3 %copy-start = (bf16[1024,2560]{1,0:T(8,128)(2,1)S(1)}, bf16[1024,2560]{1,0:T(8,128)(2,1)}, u32[]{:S(2)}) copy-start(bf16[1024,2560]{1,0:T(8,128)(2,1)} %get-tuple-element.54) | copy-start | bytes 15728644
  298.5 2.7 copy-start.3
  298.5 3.3 %copy-start.2 = (bf16[5,1024,128]{2,1,0:T(8,128)(2,1)S(1)}, bf16[5,1024,128]{2,1,0:T(8,128)(2,1)}, u32[]{:S(2)}) copy-start(bf16[5,1024,128]{2,1,0:T(8,128)(2,1)} %get-tuple-element.22) | copy-start | bytes 3932164
  298.6 4.4 %copy-start.1 = (bf16[5,1024,128]{2,1,0:T(8,128)(2,1)S(1)}, bf16[5,1024,128]{2,1,0:T(8,128)(2,1)}, u32[]{:S(2)}) copy-start(bf16[5,1024,128]{2,1,0:T(8,128)(2,1)} %get-tuple-element.23) | copy-start | bytes 3932164

commit v3 on v2

--- a/solution.py
+++ b/solution.py
@@ -33,7 +33,7 @@
     return jnp.cos(angles), jnp.sin(angles)
 
 
-def front_kernel(len_ref, cos_ref, sin_ref, g1_ref, g2_ref, x_hbm, wqkv_hbm, wo_hbm, h_hbm, n_hbm, k_ref, v_ref, xs, ns, nv, wv, acc, qv, ctx, wo, wsem, xsem, osem, hsem, nsem, ssem, rsem, *, rb, tp_size, side_size):
+def front_kernel(len_ref, cos_ref, sin_ref, g_ref, x_hbm, wqkv_hbm, wo_hbm, h_hbm, n_hbm, k_ref, v_ref, xs, ns, nv, wv, acc, qv, ctx, wo, wsem, xsem, osem, hsem, nsem, ssem, rsem, *, rb, tp_size, side_size):
     n_kind, heads, depth, head_dim = wqkv_hbm.shape
     rows = x_hbm.shape[0]
     n_blk = rows // rb
@@ -160,7 +160,7 @@
 
     def norm_step(i, carry):
         r = pl.ds(pl.multiple_of(i * nb, nb), nb)
-        nv[r, :] = rms_norm(nv[r, :], g1_ref[...])
+        nv[r, :] = rms_norm(nv[r, :], g_ref[0:1, :])
         return carry
 
     lax.fori_loop(0, rows // nb, norm_step, 0)
@@ -250,24 +250,37 @@
     for blk in range(n_blk // 2):
         c_from_left(blk).wait_recv()
         start(f_send(blk))
-    for blk in range(n_blk // 2, n_blk):
+    add_shard(0, True)
+    def pass_left(blk):
         c_from_right(blk).wait_recv()
         start(f_send(blk))
-    add_shard(0, True)
-    relay_x(2)
-    for i in range(3):
+
+    def last_hop(i):
         for kind in range(2, 4):
             x_land(i, kind).wait_recv()
         start(t_send(i, 3))
-    for i in range(3):
+
+    relay_x(2)
+    for blk in range(n_blk // 2, n_blk - 1):
+        pass_left(blk)
+    last_hop(0)
+    last_hop(1)
+    pass_left(n_blk - 1)
+    last_hop(2)
+
+    def shard_in(i):
         for j in range(4):
             t_land(i, j).wait_recv()
+
     for blk in range(n_blk // 2, n_blk):
         c_from_left(blk).wait_recv()
+    shard_in(0)
+    add_shard(-1, False)
     for blk in range(n_blk // 2):
         c_from_right(blk).wait_recv()
-    add_shard(-1, False)
+    shard_in(1)
     add_shard(1, False)
+    shard_in(2)
 
     col = pl.ds(pl.multiple_of(tp_of(2) * shard, 128), shard)
     h_copy = lambda blk: pltpu.make_async_copy(nv.at[pl.ds(blk * rb, rb), :], h_hbm.at[pl.ds(blk * rb, rb), :], hsem.at[blk])
@@ -286,7 +299,7 @@
             q = pl.ds(pl.multiple_of(i * nb, nb), nb)
             h = add_residual(xs[blk % 2, q, :], acc[r, :].astype(jnp.bfloat16))
             nv[r, :] = h
-            ns[blk % 2, q, :] = rms_norm(h, g2_ref[...])
+            ns[blk % 2, q, :] = rms_norm(h, g_ref[1:2, :])
             return carry
 
         lax.fori_loop(0, rb // nb, end_step, 0)
@@ -302,7 +315,7 @@
         copy.wait_send()
 
 
-def front_call(x, s_len, gain1, gain2, cos_full, sin_full, w_qkv, w_o, tp_size, side_size):
+def front_call(x, s_len, gains, cos_full, sin_full, w_qkv, w_o, tp_size, side_size):
     rows, depth = x.shape
     n_kind, heads, _, head_dim = w_qkv.shape
     shard = heads * head_dim
@@ -316,7 +329,7 @@
     return pl.pallas_call(
         functools.partial(front_kernel, rb=rb, tp_size=tp_size, side_size=side_size),
         out_shape=(act, act, kv, kv),
-        in_specs=[SM, VM, VM, VM, VM, ANY, ANY, ANY],
+        in_specs=[SM, VM, VM, VM, ANY, ANY, ANY],
         out_specs=(ANY, ANY, VM, VM),
         scratch_shapes=[
             pltpu.VMEM((2, rb, depth), jnp.bfloat16),
@@ -332,10 +345,10 @@
         compiler_params=pltpu.CompilerParams(vmem_limit_bytes=67043328, collective_id=0, has_side_effects=True),
         cost_estimate=pl.CostEstimate(flops=2 * rows * depth * (width + tp_size * shard), bytes_accessed=2 * (4 * rows * depth + depth * width), transcendentals=0),
         name="front",
-    )(s_len, cos_full, sin_full, gain1, gain2, x, w_qkv, w_o)
-
-
-def back_kernel(h_hbm, n_hbm, wgu_hbm, wd_hbm, k_hbm, v_hbm, tok_ref, len_ref, dcos_ref, dsin_ref, dg1_ref, dg2_ref, wqd_hbm, wod_hbm, wgud_hbm, wdd_hbm, kc_hbm, vc_hbm, out_hbm, kp_hbm, vp_hbm, dec_ref, ktok_ref, vtok_ref, nv, act, gu_v, wd_v, part, land, hb, hres, cbuf, dscr, dq, dprob, dctx, dpart, dland, dtok, dact, nsem, gsem, dsem, hsem, osem, qsem, dgsem, csem, ssem, rsem, *, fb, tp_size, side_size):
+    )(s_len, cos_full, sin_full, gains, x, w_qkv, w_o)
+
+
+def back_kernel(h_hbm, n_hbm, wgu_hbm, wd_hbm, k_hbm, v_hbm, tok_ref, len_ref, cos_ref, sin_ref, dg_ref, wqd_hbm, wod_hbm, wgud_hbm, wdd_hbm, kc_hbm, vc_hbm, out_hbm, kp_hbm, vp_hbm, dec_ref, ktok_ref, vtok_ref, nv, act, gu_v, wd_v, part, land, hb, hres, relay, cbuf, dscr, dq, dprob, dctx, dpart, dland, dtok, dact, nsem, gsem, dsem, hsem, osem, qsem, dgsem, csem, ssem, rsem, *, fb, tp_size, side_size):
     ff, depth = wd_hbm.shape
     heads, rows, head_dim = k_hbm.shape
     chunk = rows // tp_size
@@ -392,9 +405,28 @@
         slot = lax.rem(me - i + heads, heads)
         return remote(idx, src.at[i], dst.at[slot], {'tp': me, 'side': mate})
 
+    far = tp_size // 2
+    ways = ((1, k_hbm, kp_hbm), (-1, v_hbm, vp_hbm))
+
+    def far_send(n):
+        way, src, _ = ways[n]
+        return remote(n * heads + far, src.at[far], relay.at[n], {'tp': tp_of(way), 'side': mate})
+
+    def far_relay(n):
+        way, _, dst = ways[n]
+        head = tp_of(-way) * heads + far
+        return remote(2 * heads + 36 + n, relay.at[n], dst.at[head // tp_size], {'tp': tp_of(way)})
+
+    def far_land(n):
+        way, _, dst = ways[n]
+        return remote(2 * heads + 36 + n, relay.at[n], dst.at[lax.rem(me - far + heads, heads)], {'tp': tp_of(way)})
+
+    for n in range(2):
+        start(far_send(n))
     for i in range(heads):
-        start(kv_send(i, k_hbm, kp_hbm, i))
-        start(kv_send(i, v_hbm, vp_hbm, heads + i))
+        if i != far:
+            start(kv_send(i, k_hbm, kp_hbm, i))
+            start(kv_send(i, v_hbm, vp_hbm, heads + i))
     base = 2 * heads
 
     nt = (((1,), (1,)), ((), ()))
@@ -503,13 +535,13 @@
             start(rs(step + 1, way, q))
 
     def decode_qkv():
-        normed = rms_norm(tok_ref[...], dg1_ref[...])
+        normed = rms_norm(tok_ref[...], dg_ref[0:1, :])
         for kind in range(n_kind):
             for head in range(d_heads):
                 for hv in range(2):
                     wq_copy(kind, head, hv).wait()
-        cos_b = dcos_ref[...]
-        sin_b = dsin_ref[...]
+        cos_b = cos_ref[rows:rows + d_rows, :]
+        sin_b = sin_ref[rows:rows + d_rows, :]
         for kind in range(n_kind):
             c0 = kind * shard
             val = jnp.dot(normed[:, :k_half], gu_v[0, 0:k_half, c0:c0 + shard], preferred_element_type=jnp.float32)
@@ -518,7 +550,7 @@
                 one = val[:, head * head_dim:(head + 1) * head_dim]
                 if kind < 2:
                     one = one * cos_b + pltpu.roll(one, head_dim // 2, 1) * sin_b
-                (dq, ktok_ref, vtok_ref)[kind][head] = one.astype(jnp.bfloat16)
+                (dq, ktok_ref, vtok_ref)[kind][head] = one.astype(jnp.bfloat16).astype(jnp.bfloat16 if kind == 0 else jnp.float32)
 
     row_id = lax.broadcasted_iota(jnp.int32, (d_rows, 1), 0)
 
@@ -605,9 +637,10 @@
         for d in range(1, tp_size):
             d_gather_land(n, d).wait_recv()
 
-    def decode_gate_up():
-        normed = rms_norm(dtok[0], dg2_ref[...])
-        for p, (f, size) in enumerate(pieces):
+    def decode_gate_up(lo, hi):
+        normed = rms_norm(dtok[0], dg_ref[1:2, :])
+        for p in range(lo, hi):
+            f, size = pieces[p]
             gud_copy(p, 0).wait()
             gud_copy(p, 1).wait()
             gate = lax.dot_general(normed, gu_v[0, f:f + size, :], nt, preferred_element_type=jnp.float32)
@@ -624,15 +657,13 @@
     decode_qkv()
     event(0, 1)
     decode_scores()
+    event(1, 0)
+    for n in range(2):
+        far_send(n).wait_recv()
+        start(far_relay(n))
     decode_context()
     decode_scatter(0)
-    event(1, 0)
-    decode_sum(0, tok_ref)
     event(1, 1)
-    decode_gathered(0)
-    decode_gate_up()
-    decode_down()
-    decode_scatter(1)
 
     base_ag = base + 12
     h_copy.wait()
@@ -668,19 +699,28 @@
             start(ag(way, q, way))
             start(ag(way, q, 1 - way))
         if q == 0:
-            decode_sum(1, dtok.at[0])
+            decode_sum(0, tok_ref)
     own = pltpu.make_async_copy(hb, out_hbm.at[rows_of(0), :], osem.at[0])
     own.start()
+    decode_gathered(0)
+    mid = len(pieces) // 2
     for q in range(2):
         for way in range(2):
             ag_land(way, q, way).wait_recv()
             start(fwd(way, q))
+        decode_gate_up(q * mid, mid if q == 0 else len(pieces))
+    decode_down()
+    decode_scatter(1)
+    decode_sum(1, dtok.at[0])
     for q in range(2):
         for way in range(2):
             ag_land(way, q, 1 - way).wait_recv()
     for i in range(heads):
-        kv_land(i, k_hbm, kp_hbm, i).wait_recv()
-        kv_land(i, v_hbm, vp_hbm, heads + i).wait_recv()
+        if i != far:
+            kv_land(i, k_hbm, kp_hbm, i).wait_recv()
+            kv_land(i, v_hbm, vp_hbm, heads + i).wait_recv()
+    for n in range(2):
+        far_land(n).wait_recv()
     for q in range(2):
         for way in range(2):
             fwd_land(way, q).wait_recv()
@@ -698,17 +738,17 @@
     chunk = rows // tp_size
     fb = 256
     n_piece = -(-ff // fb)
-    n_msg = 2 * heads + 12 + 12 + 12
+    n_msg = 2 * heads + 12 + 12 + 12 + 2
     d_rows = dec[0].shape[0]
     head_dim = k.shape[2]
-    cache_len = dec[10].shape[2]
+    cache_len = dec[9].shape[2]
     dma = pltpu.SemaphoreType.DMA
     bf16 = jnp.bfloat16
     kv = jax.ShapeDtypeStruct(k.shape, bf16)
     return pl.pallas_call(
         functools.partial(back_kernel, fb=fb, tp_size=tp_size, side_size=side_size),
-        out_shape=(jax.ShapeDtypeStruct((rows, depth), bf16), kv, kv, jax.ShapeDtypeStruct((d_rows, depth), bf16)) + (jax.ShapeDtypeStruct((heads, d_rows, head_dim), bf16),) * 2,
-        in_specs=[ANY] * 6 + [VM] * 6 + [ANY] * 6,
+        out_shape=(jax.ShapeDtypeStruct((rows, depth), bf16), kv, kv, jax.ShapeDtypeStruct((d_rows, depth), bf16)) + (jax.ShapeDtypeStruct((heads, d_rows, head_dim), jnp.float32),) * 2,
+        in_specs=[ANY] * 6 + [VM] * 5 + [ANY] * 6,
         out_specs=(ANY,) * 3 + (VM,) * 3,
         scratch_shapes=[
             pltpu.VMEM((rows, depth), bf16),
@@ -719,6 +759,7 @@
             pltpu.VMEM((3, chunk, depth), jnp.float32),
             pltpu.VMEM((chunk, depth), bf16),
             pltpu.VMEM((chunk, depth), bf16),
+            pltpu.VMEM((2, rows, head_dim), bf16),
             pltpu.VMEM((2, heads, cache_len, head_dim), bf16),
             pltpu.VMEM((heads, d_rows, cache_len), jnp.float32),
             pltpu.VMEM((heads, d_rows, head_dim), bf16),
@@ -736,10 +777,33 @@
     )(h, normed, w_gu, w_down, k, v, *dec)
 
 
-def write_cache(cache, new, at):
-    row_count, cache_len = cache.shape[:2]
-    here = (jnp.arange(cache_len)[None, :] == at[:, None])[:, :, None, None, None]
-    return jnp.where(here, new.transpose(1, 0, 2)[:, None, :, None, :], cache)
+def cache_kernel(len_ref, kt_ref, vt_ref, k_ref, v_ref, ko_ref, vo_ref):
+    n_rows, heads, cache_len, head_dim = k_ref.shape
+    first = pl.program_id(0) * n_rows
+    pos = lax.broadcasted_iota(jnp.int32, (cache_len, head_dim), 0)
+    for j in range(n_rows):
+        here = pos == len_ref[first + j]
+        for head in range(heads):
+            for tok, src, dst in ((kt_ref, k_ref, ko_ref), (vt_ref, v_ref, vo_ref)):
+                new = tok[head, pl.ds(first + j, 1), :]
+                dst[j, head] = jnp.where(here, new, src[j, head].astype(jnp.float32)).astype(dst.dtype)
+
+
+def cache_call(c_len, k_tok, v_tok, k_cache, v_cache):
+    d_rows, heads, cache_len, head_dim = k_cache.shape
+    step = 2
+    block = pl.BlockSpec((step, heads, cache_len, head_dim), lambda i: (i, 0, 0, 0))
+    out = jax.ShapeDtypeStruct(k_cache.shape, k_cache.dtype)
+    return pl.pallas_call(
+        cache_kernel,
+        grid=(d_rows // step,),
+        out_shape=(out, out),
+        in_specs=[SM, VM, VM, block, block],
+        out_specs=(block, block),
+        compiler_params=pltpu.CompilerParams(vmem_limit_bytes=67043328),
+        cost_estimate=pl.CostEstimate(flops=k_cache.size, bytes_accessed=8 * k_cache.size, transcendentals=0),
+        name="cache",
+    )(c_len, k_tok, v_tok, k_cache, v_cache)
 
 
 def run_layers(prompt, s_len, pre, tokens, k_cache, v_cache, c_len, dec, tp_size, side_size):
@@ -750,21 +814,20 @@
     shard = heads_loc * head_dim
     d_rows, cache_len = k_cache.shape[1:3]
 
-    def full_tables(positions):
-        cos_tab, sin_tab = rope_tables(positions, head_dim)
-        return jnp.concatenate([cos_tab, cos_tab], axis=-1), jnp.concatenate([-sin_tab, sin_tab], axis=-1)
-
-    cos_full, sin_full = full_tables(jnp.arange(rows))
-    d_cos, d_sin = full_tables(c_len)
+    cos_tab, sin_tab = rope_tables(jnp.concatenate([jnp.arange(rows, dtype=jnp.int32), c_len]), head_dim)
+    cos_full = jnp.concatenate([cos_tab, cos_tab], axis=-1)
+    sin_full = jnp.concatenate([-sin_tab, sin_tab], axis=-1)
     hidden = prompt
     outs = []
     for layer in range(layers):
         w_t = w_qkv[layer].transpose(1, 2, 0, 3)
-        hidden, normed, k, v = front_call(hidden, s_len, gains[layer, 0][None], gains[layer, 1][None], cos_full, sin_full, w_t, w_out[layer].reshape(shard, width), tp_size, side_size)
+        hidden, normed, k, v = front_call(hidden, s_len, gains[layer], cos_full, sin_full, w_t, w_out[layer].reshape(shard, width), tp_size, side_size)
         by_head = lambda cache: cache[layer].reshape(d_rows, cache_len, heads_loc, head_dim).transpose(0, 2, 1, 3)
-        dec_args = (tokens, c_len[:, None], d_cos, d_sin, dgains[layer, 0][None], dgains[layer, 1][None], dw_qkv[layer].reshape(width, 3, heads_loc, head_dim).transpose(1, 2, 0, 3), dw_out[layer].reshape(shard, width), dw_gu[layer], dw_down[layer], by_head(k_cache), by_head(v_cache))
+        dec_args = (tokens, c_len[:, None], cos_full, sin_full, dgains[layer], dw_qkv[layer].reshape(width, 3, heads_loc, head_dim).transpose(1, 2, 0, 3), dw_out[layer].reshape(shard, width), dw_gu[layer], dw_down[layer], by_head(k_cache), by_head(v_cache))
         hidden, k_inst, v_inst, tokens, k_tok, v_tok = back_call(hidden, normed, w_gu[layer], w_down[layer], k, v, dec_args, tp_size, side_size)
-        outs.append((k_inst.transpose(1, 0, 2)[:, :, None, :], v_inst.transpose(1, 0, 2)[:, :, None, :], write_cache(k_cache[layer], k_tok, c_len), write_cache(v_cache[layer], v_tok, c_len)))
+        k_new, v_new = cache_call(c_len, k_tok, v_tok, by_head(k_cache), by_head(v_cache))
+        as_cache = lambda new: new.transpose(0, 2, 1, 3)[:, :, :, None, :]
+        outs.append((k_inst.transpose(1, 0, 2)[:, :, None, :], v_inst.transpose(1, 0, 2)[:, :, None, :], as_cache(k_new), as_cache(v_new)))
     return (hidden, tokens) + tuple(jnp.stack(parts) for parts in zip(*outs))
 
 

time: 308 us -> 288 us (0.935)
  the two profiles are of different devices: /device:TPU:97 before, /device:TPU:96 now
where the time goes in v3:
time: 288 us; the launch traced here: 284 us
  Pallas kernels  269 us (93%)
  local copies, waits for them, and re-layouts  9.43 us (3%)
  other arithmetic  3.92 us (1%)
    pallas_call x1, Pallas kernels, back_call(): pl.pallas_call(functools.partial(back_kernel, fb=fb, tp_size=tp_size, sid...  177 us
    pallas_call x1, Pallas kernels, front_call(): pl.pallas_call(functools.partial(front_kernel, rb=rb, tp_size=tp_size, si...  81.3 us
    pallas_call x1, Pallas kernels, cache_call(): pl.pallas_call(cache_kernel, grid=(d_rows // step,), out_shape=(out, out)...  10.7 us
    unnamed x10, local copies, waits for them, and re-layouts  8.1 us

profile of v3, /device:TPU:96, one launch (start us, length us, event | category | flops | bytes accessed | tf_op | source)
XLA Modules:
  0.0 283.7 jit_solution(2490580774351108950)
XLA Ops:
  1.3 0.7 add_convert_fusion
  2.0 1.3 copy.22.len_ref
  3.3 1.9 fusion
  5.2 1.3 pad_maximum_fusion
  6.5 81.3 %front.1 = (bf16[1024,2560]{1,0:T(8,128)(2,1)}, bf16[1024,2560]{1,0:T(8,128)(2,1)}, bf16[5,1024,128]{2,1,0:T(8,128)(2,1)}, bf16[5,1024,128]{2,1,0:T(8,128)(2,1)}) custom-call(s32[1]{0:T(128)S(6)} %copy.31.len_ref, f32[1040,128]{1,0:T(8,128)} %get-tuple-element.39.cos_ref, f32[1040,128]{1,0:T(8,128)} %get-tuple-element.40.sin_ref, f32[2,2560]{1,0:T(2,128)} %bitcast.58, ...), custom_call_target="tpu_custom_call" | custom-call | flops 23488102400 | bytes 30801920 | tf_op jit(solution)/shard_map/front/pallas_call | solution.py:329
  87.8 176.8 %back.1 = (bf16[1024,2560]{1,0:T(8,128)(2,1)}, bf16[5,1024,128]{2,1,0:T(8,128)(2,1)}, bf16[5,1024,128]{2,1,0:T(8,128)(2,1)}, bf16[16,2560]{1,0:T(8,128)(2,1)}, f...) custom-call(bf16[1024,2560]{1,0:T(8,128)(2,1)} %get-tuple-element.18.h_hbm, bf16[1024,2560]{1,0:T(8,128)(2,1)} %get-tuple-element.19.n_hbm, ...), custom_call_target="tpu_custom_call" | custom-call | flops 27179089920 | bytes 47513600 | tf_op jit(solution)/shard_map/back/pallas_call | solution.py:748
  264.6 10.7 %cache.1 = (bf16[16,5,256,128]{3,2,1,0:T(8,128)(2,1)}, bf16[16,5,256,128]{3,2,1,0:T(8,128)(2,1)}) custom-call(s32[16]{0:T(128)} %len_ref.2, f32[5,16,128]{2,1,0:T(8,128)} %get-tuple-element.26.kt_ref, f32[5,16,128]{2,1,0:T(8,128)} %get-tuple-element.27.vt_ref, bf16[16,5,256,128]{3,2,1,0:T(8,128)(2,1)} %bitcast.42, bf16[16,5,256,128]{3,2,1,0:T(8,128)(2,1)} %bitcast.44), custom_call_target="tpu_custom_call" | custom-call | flops 2621440 | bytes 20971520 | tf_op jit(solution)/shard_map/cache/pallas_call | solution.py:797
  275.4 0.0 copy-start.2
  275.4 0.0 copy-start.1
  275.4 0.0 copy-start
  275.4 5.3 %copy.32 = bf16[1024,2560]{1,0:T(8,128)(2,1)} copy(bf16[1024,2560]{1,0:T(8,128)(2,1)} %get-tuple-element.47) | data formatting | bytes 10485760
  280.7 0.0 copy-done.2
  280.7 0.6 copy.33
  281.4 0.0 copy-done.1
  281.4 1.1 copy.34
  282.4 0.0 copy-done
  282.4 1.1 copy.35
  (2 shorter events, 0.0 us)
Async XLA Ops:
  275.4 5.4 %copy-start.2 = (bf16[16,2560]{1,0:T(8,128)(2,1)S(1)}, bf16[16,2560]{1,0:T(8,128)(2,1)}, u32[]{:S(2)}) copy-start(bf16[16,2560]{1,0:T(8,128)(2,1)} %get-tuple-element.48) | copy-start | bytes 245764
  275.4 6.0 %copy-start.1 = (bf16[5,1024,128]{2,1,0:T(8,128)(2,1)S(1)}, bf16[5,1024,128]{2,1,0:T(8,128)(2,1)}, u32[]{:S(2)}) copy-start(bf16[5,1024,128]{2,1,0:T(8,128)(2,1)} %get-tuple-element.24) | copy-start | bytes 3932164
  275.4 7.0 %copy-start = (bf16[5,1024,128]{2,1,0:T(8,128)(2,1)S(1)}, bf16[5,1024,128]{2,1,0:T(8,128)(2,1)}, u32[]{:S(2)}) copy-start(bf16[5,1024,128]{2,1,0:T(8,128)(2,1)} %get-tuple-element.25) | copy-start | bytes 3932164

commit v4 on v3

--- a/solution.py
+++ b/solution.py
@@ -780,13 +780,19 @@
 def cache_kernel(len_ref, kt_ref, vt_ref, k_ref, v_ref, ko_ref, vo_ref):
     n_rows, heads, cache_len, head_dim = k_ref.shape
     first = pl.program_id(0) * n_rows
-    pos = lax.broadcasted_iota(jnp.int32, (cache_len, head_dim), 0)
+    tile = 16
+    pos = lax.broadcasted_iota(jnp.int32, (tile, head_dim), 0)
+    ko_ref[...] = k_ref[...]
+    vo_ref[...] = v_ref[...]
     for j in range(n_rows):
-        here = pos == len_ref[first + j]
+        at = len_ref[first + j]
+        base = pl.multiple_of(at // tile * tile, tile)
+        here = pos == at - base
         for head in range(heads):
             for tok, src, dst in ((kt_ref, k_ref, ko_ref), (vt_ref, v_ref, vo_ref)):
                 new = tok[head, pl.ds(first + j, 1), :]
-                dst[j, head] = jnp.where(here, new, src[j, head].astype(jnp.float32)).astype(dst.dtype)
+                old = src[j, head, pl.ds(base, tile), :].astype(jnp.float32)
+                dst[j, head, pl.ds(base, tile), :] = jnp.where(here, new, old).astype(dst.dtype)
 
 
 def cache_call(c_len, k_tok, v_tok, k_cache, v_cache):

time: 288 us -> 287 us (level)
  no operation moved by 1% of the time
where the time goes in v4:
time: 287 us; the launch traced here: 283 us
  Pallas kernels  268 us (93%)
  local copies, waits for them, and re-layouts  9.43 us (3%)
  other arithmetic  3.92 us (1%)
    pallas_call x1, Pallas kernels, back_call(): pl.pallas_call(functools.partial(back_kernel, fb=fb, tp_size=tp_size, sid...  177 us
    pallas_call x1, Pallas kernels, front_call(): pl.pallas_call(functools.partial(front_kernel, rb=rb, tp_size=tp_size, si...  81.3 us
    pallas_call x1, Pallas kernels, cache_call(): pl.pallas_call(cache_kernel, grid=(d_rows // step,), out_shape=(out, out)...  10.2 us
    unnamed x10, local copies, waits for them, and re-layouts  8.1 us

profile of v4, /device:TPU:96, one launch (start us, length us, event | category | flops | bytes accessed | tf_op | source)
XLA Modules:
  0.0 283.2 jit_solution(13771658381175992270)
XLA Ops:
  1.3 0.7 add_convert_fusion
  2.0 1.3 copy.22.len_ref
  3.3 1.9 fusion
  5.2 1.3 pad_maximum_fusion
  6.5 81.3 %front.1 = (bf16[1024,2560]{1,0:T(8,128)(2,1)}, bf16[1024,2560]{1,0:T(8,128)(2,1)}, bf16[5,1024,128]{2,1,0:T(8,128)(2,1)}, bf16[5,1024,128]{2,1,0:T(8,128)(2,1)}) custom-call(s32[1]{0:T(128)S(6)} %copy.31.len_ref, f32[1040,128]{1,0:T(8,128)} %get-tuple-element.39.cos_ref, f32[1040,128]{1,0:T(8,128)} %get-tuple-element.40.sin_ref, f32[2,2560]{1,0:T(2,128)} %bitcast.58, ...), custom_call_target="tpu_custom_call" | custom-call | flops 23488102400 | bytes 30801920 | tf_op jit(solution)/shard_map/front/pallas_call | solution.py:329
  87.8 176.8 %back.1 = (bf16[1024,2560]{1,0:T(8,128)(2,1)}, bf16[5,1024,128]{2,1,0:T(8,128)(2,1)}, bf16[5,1024,128]{2,1,0:T(8,128)(2,1)}, bf16[16,2560]{1,0:T(8,128)(2,1)}, f...) custom-call(bf16[1024,2560]{1,0:T(8,128)(2,1)} %get-tuple-element.18.h_hbm, bf16[1024,2560]{1,0:T(8,128)(2,1)} %get-tuple-element.19.n_hbm, ...), custom_call_target="tpu_custom_call" | custom-call | flops 27179089920 | bytes 47513600 | tf_op jit(solution)/shard_map/back/pallas_call | solution.py:748
  264.6 10.2 %cache.1 = (bf16[16,5,256,128]{3,2,1,0:T(8,128)(2,1)}, bf16[16,5,256,128]{3,2,1,0:T(8,128)(2,1)}) custom-call(s32[16]{0:T(128)} %len_ref.2, f32[5,16,128]{2,1,0:T(8,128)} %get-tuple-element.26.kt_ref, f32[5,16,128]{2,1,0:T(8,128)} %get-tuple-element.27.vt_ref, bf16[16,5,256,128]{3,2,1,0:T(8,128)(2,1)} %bitcast.42, bf16[16,5,256,128]{3,2,1,0:T(8,128)(2,1)} %bitcast.44), custom_call_target="tpu_custom_call" | custom-call | flops 2621440 | bytes 20971520 | tf_op jit(solution)/shard_map/cache/pallas_call | solution.py:803
  274.8 0.0 copy-start.2
  274.8 0.0 copy-start.1
  274.8 0.0 copy-start
  274.8 5.3 %copy.32 = bf16[1024,2560]{1,0:T(8,128)(2,1)} copy(bf16[1024,2560]{1,0:T(8,128)(2,1)} %get-tuple-element.47) | data formatting | bytes 10485760
  280.2 0.0 copy-done.2
  280.2 0.6 copy.33
  280.8 0.0 copy-done.1
  280.8 1.1 copy.34
  281.9 0.0 copy-done
  281.9 1.1 copy.35
  (2 shorter events, 0.0 us)
Async XLA Ops:
  274.8 5.4 %copy-start.2 = (bf16[16,2560]{1,0:T(8,128)(2,1)S(1)}, bf16[16,2560]{1,0:T(8,128)(2,1)}, u32[]{:S(2)}) copy-start(bf16[16,2560]{1,0:T(8,128)(2,1)} %get-tuple-element.48) | copy-start | bytes 245764
  274.8 6.0 %copy-start.1 = (bf16[5,1024,128]{2,1,0:T(8,128)(2,1)S(1)}, bf16[5,1024,128]{2,1,0:T(8,128)(2,1)}, u32[]{:S(2)}) copy-start(bf16[5,1024,128]{2,1,0:T(8,128)(2,1)} %get-tuple-element.24) | copy-start | bytes 3932164
  274.8 7.0 %copy-start = (bf16[5,1024,128]{2,1,0:T(8,128)(2,1)S(1)}, bf16[5,1024,128]{2,1,0:T(8,128)(2,1)}, u32[]{:S(2)}) copy-start(bf16[5,1024,128]{2,1,0:T(8,128)(2,1)} %get-tuple-element.25) | copy-start | bytes 3932164
